TPU v7x, 32 devices: a whole 2x2x4 slice. The times are simulated.
32 devices in a mesh: row: 16 (over z, y, core), col: 2 (over x).
Axes of the slice: x: 2, y: 2, z: 4, core: 2. Of those that a mesh axis runs over, the one named last changes fastest.
Arguments:
- features: bfloat16 [256, 128, 384], P('row', 'col'), may hold values from -30 to 30
- inner_weights: bfloat16 [4, 3, 3, 384, 384], replicated, may hold values from -0.109375 to 0.109375
- far_weights: bfloat16 [3, 3, 384, 384], replicated, may hold values from -0.109375 to 0.109375
- gains: float32 [5, 384], replicated, may hold values from 0.1 to 1.9
Outputs:
- result: float32 [256, 128, 384], P('row', 'col')
All inputs are finite; a program needn't handle non-finite values.
Results may differ from a plain program's by a relative error of at most 0.0024.
Values may be sent and summed in bfloat16 or wider, within the bound.
No kernel may reach another device: no remote copies, remote signals or barrier semaphores. Data moves between devices by JAX's collectives and lax.ppermute only.
A program may use at most 192 MiB of HBM per device.

v0:
```python
import functools

import jax
import jax.numpy as jnp
from jax import lax
from jax.experimental import pallas as pl
from jax.experimental.pallas import tpu as pltpu
from jax.sharding import PartitionSpec as P

FAR = 64
DILATIONS = (1, 2, 4, 8)
PAD = 8
VMEM_LIMIT = 40 * 1024 * 1024


def normed(stream, gain):
    centre = jnp.mean(stream, axis=-1, keepdims=True)
    moved = stream - centre
    spread = jnp.mean(moved * moved, axis=-1, keepdims=True)
    return jax.nn.gelu(moved * lax.rsqrt(spread + 1e-05) * gain)


def spread_taps(line_ref, taps_ref, row, dilation, start, cols):
    ch = line_ref.shape[-1]
    for tap in range(3):
        shift = (tap - 1) * dilation
        taps_ref[row, :, tap * ch : (tap + 1) * ch] = line_ref[row, pl.ds(start + shift, cols), :].astype(
            taps_ref.dtype
        )


def clear_edges(line_ref):
    rows, width, ch = line_ref.shape
    line_ref[:, 0:PAD, :] = jnp.zeros((rows, PAD, ch), line_ref.dtype)
    line_ref[:, width - PAD : width, :] = jnp.zeros((rows, PAD, ch), line_ref.dtype)


def conv_part(taps_ref, weight_ref, first, rows, dilation, taps=(0, 1, 2)):
    cols, depth = taps_ref.shape[1:]
    lhs = [taps_ref[first + tap * dilation : first + tap * dilation + rows].reshape(rows * cols, depth) for tap in taps]
    lhs = lhs[0] if len(lhs) == 1 else jnp.concatenate(lhs, axis=1)
    weight = weight_ref[taps[0] * depth : (taps[-1] + 1) * depth, :]
    out = jnp.dot(lhs, weight, preferred_element_type=jnp.float32)
    return out.reshape(rows, cols, out.shape[-1])


def in_grid(col_lo, col_hi, value):
    cols = lax.broadcasted_iota(jnp.int32, value.shape, 0)
    keep = (cols >= col_lo) & (cols < col_hi)
    return jnp.where(keep, value, 0.0)


class Plan:
    def __init__(self, tile_rows, tile_cols, ch, n_row, n_col):
        self.tile_rows, self.tile_cols, self.ch = tile_rows, tile_cols, ch
        self.n_row, self.n_col = n_row, n_col
        self.two = n_col == 2
        self.ext = -(-sum(DILATIONS) // 16) * 16
        self.width = tile_cols + (self.ext if self.two else 2 * self.ext)
        self.last = DILATIONS[-1]
        self.width4 = tile_cols + (self.last if self.two else 2 * self.last)

    def own(self, col):
        return pl.multiple_of(col * self.ext, 8) if self.two else self.ext

    def own4(self, col):
        return pl.multiple_of(col * self.last, 8) if self.two else self.last

    def start4(self, col):
        return pl.multiple_of(col * (self.ext - self.last), 8) if self.two else self.ext - self.last

    def sides(self, col):
        if self.two:
            return (pl.multiple_of((1 - col) * self.tile_cols, 8),)
        return (0, self.ext + self.tile_cols)

    def col_range(self, col):
        if self.two:
            return 0, self.width
        lo = jnp.where(col == 0, self.ext, 0)
        hi = jnp.where(col == self.n_col - 1, self.ext + self.tile_cols, self.width)
        return lo, hi

    def inside(self, col, value):
        if self.two:
            return value
        return in_grid(*self.col_range(col), value)

    def starts(self, row_id, span):
        last = self.tile_rows - span
        one = jnp.where(row_id % 2 == 0, last, 0)
        return one, last - one


def lay(line, taps, row, value, dilation, start, cols):
    width = value.shape[0]
    line[row, PAD : PAD + width, :] = value
    spread_taps(line, taps, row, dilation, start, cols)


def rows_of(count, body, step=4):
    def block(k, _):
        for j in range(step):
            body(k * step + j)
        return 0

    lax.fori_loop(0, count // step, block, 0)
    for row in range(count // step * step, count):
        body(row)


def gather_rows(plan, halo, features, *refs):
    n_side = 1 if plan.two else 2
    sides, outs, (sems,) = refs[:n_side], refs[n_side : n_side + 2], refs[n_side + 2 :]
    row_id, col = lax.axis_index("row"), lax.axis_index("col")
    copies = []
    for out, start in zip(outs, plan.starts(row_id, halo)):
        for part, offset in zip((features,) + sides, (plan.own(col),) + plan.sides(col)):
            copies.append(
                pltpu.make_async_copy(
                    part.at[pl.ds(start, halo)],
                    out.at[:, pl.ds(offset, part.shape[1])],
                    sems.at[len(copies)],
                )
            )
    for copy in copies:
        copy.start()
    for copy in copies:
        copy.wait()


CHUNK = 4


def one_own(plan, halo, *refs):
    n_side = 1 if plan.two else 2
    parts = refs[: 1 + n_side]
    w_hbm, gains, mid, mid_act, edge_act, edge_base, base, line, taps, weight, sem = refs[1 + n_side :]
    col = lax.axis_index("col")
    copy = pltpu.make_async_copy(w_hbm.at[0], weight, sem)
    copy.start()
    rows, width = plan.tile_rows, plan.width
    for part, offset in zip(parts, (plan.own(col),) + plan.sides(col)):
        base[:, pl.ds(offset, part.shape[1]), :] = part[...].astype(jnp.float32)
    clear_edges(line)

    def prepare(row):
        lay(line, taps, row, plan.inside(col, normed(base[row], gains[0:1, :])), DILATIONS[0], PAD, width)

    def follow(row):
        mid_act[row] = plan.inside(col, normed(mid[row], gains[1:2, :])).astype(mid_act.dtype)

    lead = 2 * CHUNK
    rows_of(lead, prepare)
    copy.wait()
    edge = DILATIONS[1]
    count = mid.shape[0] // CHUNK
    for k in range(count):
        at = k * CHUNK
        mid[at : at + CHUNK] = base[edge + at : edge + at + CHUNK] + conv_part(
            taps, weight, edge + at - DILATIONS[0], CHUNK, DILATIONS[0]
        )
        for row in range(lead + at, min(lead + at + CHUNK, rows)):
            prepare(row)
        if k:
            for row in range(at - CHUNK, at):
                follow(row)
    ch = plan.ch
    for k, first in enumerate((0, rows - halo)):
        edge_act[k * halo : (k + 1) * halo] = taps[first : first + halo, :, ch : 2 * ch]
        edge_base[k * halo : (k + 1) * halo] = base[first : first + halo]
    rows_of(CHUNK, lambda row: follow((count - 1) * CHUNK + row))


def one_two(plan, halo, *refs):
    got, refs = refs[:2], refs[2:]
    mid, mid_act, edge_act, edge_base, w_hbm, gains, stream, act, send_one, send_two = refs[:10]
    base, line, taps_one, rim, taps_two, w_one, w_two, sems = refs[10:]
    row_id, col = lax.axis_index("row"), lax.axis_index("col")
    copies = [pltpu.make_async_copy(w_hbm.at[k], w, sems.at[k]) for k, w in enumerate((w_one, w_two))]
    for copy in copies:
        copy.start()
    rows, width, ch = plan.tile_rows, plan.width, plan.ch
    d_one, d_two = DILATIONS[:2]
    clear_edges(line)
    base[halo : 3 * halo] = edge_base[...]
    top = (halo * 3) * (1 - row_id % 2)
    for ref, at in zip(got, (top, 3 * halo - top)):
        base[pl.ds(at, halo)] = ref[...].astype(jnp.float32)
    for row in range(2 * halo):
        lay(line, taps_one, halo + row, edge_act[row].astype(jnp.float32), d_one, PAD, width)
    for row in tuple(range(halo)) + tuple(range(3 * halo, 4 * halo)):
        lay(line, taps_one, row, plan.inside(col, normed(base[row], gains[0:1, :])), d_one, PAD, width)
    n_mid = mid.shape[0]

    def spread_mid(row):
        lay(line, taps_two, 2 * d_two + row, mid_act[row].astype(jnp.float32), d_two, PAD, width)

    copies[0].wait()
    for k in range(2):
        at = 2 * halo * k
        rim[k * CHUNK : (k + 1) * CHUNK] = base[at + 1 : at + 1 + CHUNK] + conv_part(taps_one, w_one, at, CHUNK, d_one)
        for row in range(k * n_mid // 2, (k + 1) * n_mid // 2):
            spread_mid(row)
    copies[1].wait()

    def spread_rim(row):
        value = plan.inside(col, normed(rim[row], gains[1:2, :]))
        if row < d_two:
            value = jnp.where(row_id == 0, 0.0, value)
        if row >= 2 * CHUNK - d_two:
            value = jnp.where(row_id == plan.n_row - 1, 0.0, value)
        lay(line, taps_two, row if row < CHUNK else n_mid + row, value, d_two, PAD, width)

    def finish(row):
        act[row] = plan.inside(col, normed(stream[row], gains[2:3, :])).astype(act.dtype)

    def second(first):
        return conv_part(taps_two, w_two, first, CHUNK, d_two)

    inner = tuple(range(CHUNK, rows - CHUNK, CHUNK))
    per = -(-2 * CHUNK // len(inner))
    for k, first in enumerate(inner):
        stream[first : first + CHUNK] = mid[first - d_two : first - d_two + CHUNK] + second(first)
        for row in range(k * per, min((k + 1) * per, 2 * CHUNK)):
            spread_rim(row)
    out = second(0)
    stream[0:d_two] = rim[d_two : 2 * d_two] + out[:d_two]
    stream[d_two:CHUNK] = mid[0 : CHUNK - d_two] + out[d_two:]
    for first in inner[: len(inner) // 2]:
        for row in range(first, first + CHUNK):
            finish(row)
    last = rows - CHUNK
    out = second(last)
    stream[last : last + d_two] = mid[n_mid - d_two : n_mid] + out[:d_two]
    stream[last + d_two : rows] = rim[CHUNK : CHUNK + d_two] + out[d_two:]
    for first in inner[len(inner) // 2 :]:
        for row in range(first, first + CHUNK):
            finish(row)
    rows_of(CHUNK, finish)
    rows_of(CHUNK, lambda row: finish(last + row))
    for ref, at in zip((send_one, send_two), plan.starts(row_id, DILATIONS[2])):
        ref[...] = act[pl.ds(at, DILATIONS[2])]


def three_own(plan, act, w_hbm, stream, gains, edge, mid, mid_act, line, taps, full, row_act, weight, sem):
    col = lax.axis_index("col")
    copy = pltpu.make_async_copy(w_hbm.at[2], weight, sem)
    copy.start()
    d = DILATIONS[2]
    rows, width = plan.tile_rows, plan.width
    clear_edges(line)
    rows_of(rows, lambda row: lay(line, taps, row, act[row].astype(jnp.float32), d, PAD, width))
    copy.wait()
    for first in range(d, rows - d, CHUNK):
        full[first - d : first - d + CHUNK] = stream[first : first + CHUNK] + conv_part(taps, weight, first - d, CHUNK, d)

    def finish(row):
        emit(plan, col, full, row_act, row, gains[3:4, :], mid, mid_act, row)

    count = rows - 2 * d
    edge[0:d] = stream[0:d] + conv_part(taps, weight, -d, d, d, (1, 2))
    for row in range(count // 2):
        finish(row)
    edge[d : 2 * d] = stream[rows - d : rows] + conv_part(taps, weight, rows - 2 * d, d, d, (0, 1))
    for row in range(count // 2, count):
        finish(row)


def emit(plan, col, full, row_act, row, gain, stream, act, at):
    row_act[row] = plan.inside(col, normed(full[row], gain))
    act[at] = row_act[row, pl.ds(plan.start4(col), plan.width4), :].astype(act.dtype)
    stream[at] = full[row, pl.ds(plan.own(col), plan.tile_cols), :]


def partner_weights(plan, row_id, w_hbm, layer, weight, sems):
    depth = weight.shape[1]
    one = jnp.where(row_id % 2 == 0, 2 * depth, 0)
    return [
        pltpu.make_async_copy(
            w_hbm.at[layer, pl.ds(pl.multiple_of(at, 16), depth)], weight.at[k], sems.at[k]
        )
        for k, at in enumerate((one, 2 * depth - one))
    ]


def three_rim(plan, got_one, got_two, edge, mid, mid_act, w_hbm, gains, stream, act, send_one, send_two, *scratch):
    line, taps, weight, full, row_act, sems = scratch
    row_id, col = lax.axis_index("row"), lax.axis_index("col")
    copies = partner_weights(plan, row_id, w_hbm, 2, weight, sems)
    for copy in copies:
        copy.start()
    d = DILATIONS[2]
    rows, width = plan.tile_rows, plan.width
    clear_edges(line)
    for k, ref in enumerate((got_one, got_two)):
        for row in range(d):
            lay(line, taps, k * d + row, ref[row].astype(jnp.float32), d, PAD, width)
    stream[d : rows - d] = mid[...]
    act[d : rows - d] = mid_act[...]
    at_one, at_two = plan.starts(row_id, d)
    half = jnp.where(row_id % 2 == 0, d, 0)
    for k, (place, at) in enumerate(((half, at_one), (d - half, at_two))):
        copies[k].wait()
        full[k * d : (k + 1) * d] = edge[pl.ds(place, d)] + conv_part(taps, weight.at[k], k * d, d, d, (0,))
    for k, at in enumerate((at_one, at_two)):
        for row in range(d):
            emit(plan, col, full, row_act, k * d + row, gains[3:4, :], stream, act, at + row)
    for ref, at in zip((send_one, send_two), plan.starts(row_id, DILATIONS[3])):
        ref[...] = act[pl.ds(at, DILATIONS[3])]


def four_own(plan, act, w_hbm, stream, out, line, taps, weight, sem):
    col = lax.axis_index("col")
    copy = pltpu.make_async_copy(w_hbm.at[3], weight, sem)
    copy.start()
    d = DILATIONS[3]
    rows, cols = plan.tile_rows, plan.tile_cols
    start = PAD + plan.own4(col)
    clear_edges(line)
    rows_of(rows, lambda row: lay(line, taps, row, act[row].astype(jnp.float32), d, start, cols))
    copy.wait()
    for first in range(0, rows, CHUNK):
        used = tuple(t for t in range(3) if 0 <= first + (t - 1) * d < rows)
        out[first : first + CHUNK] = stream[first : first + CHUNK] + conv_part(taps, weight, first - d, CHUNK, d, used)


def four_rim(plan, got_one, got_two, acc, w_hbm, gains, stream, act_a, act_b, line, taps, weight, sems):
    row_id, col = lax.axis_index("row"), lax.axis_index("col")
    copies = partner_weights(plan, row_id, w_hbm, 3, weight, sems)
    for copy in copies:
        copy.start()
    d = DILATIONS[3]
    rows, cols = plan.tile_rows, plan.tile_cols
    start = PAD + plan.own4(col)
    clear_edges(line)
    for k, ref in enumerate((got_one, got_two)):
        rows_of(d, lambda row, k=k, ref=ref: lay(line, taps, k * d + row, ref[row].astype(jnp.float32), d, start, cols))
    if rows > 2 * d:
        stream[d : rows - d] = acc[d : rows - d]
    pending = []
    for k, at in enumerate(plan.starts(row_id, d)):
        copies[k].wait()
        for step in range(0, d, CHUNK):
            stream[pl.ds(at + step, CHUNK)] = acc[pl.ds(at + step, CHUNK)] + conv_part(
                taps, weight.at[k], k * d + step, CHUNK, d, (0,)
            )
    half = rows // 2
    for k, act in enumerate((act_a, act_b)):

        def finish(row, act=act, k=k):
            act[row] = normed(stream[k * half + row], gains[4:5, :]).astype(act.dtype)

        rows_of(half, finish)


def times(a, w):
    rows, cols, ch = a.shape
    return jnp.dot(a.reshape(rows * cols, ch), w, preferred_element_type=jnp.float32).reshape(rows, cols, ch)


def call(kernel, out_shape, scratch, args, flops, any_args=()):
    return pl.pallas_call(
        kernel,
        out_shape=out_shape,
        in_specs=[
            pl.BlockSpec(memory_space=pl.ANY) if k in any_args else pl.BlockSpec(memory_space=pltpu.VMEM)
            for k in range(len(args))
        ],
        out_specs=jax.tree.map(lambda _: pl.BlockSpec(memory_space=pltpu.VMEM), out_shape),
        scratch_shapes=scratch,
        compiler_params=pltpu.CompilerParams(vmem_limit_bytes=VMEM_LIMIT),
        cost_estimate=pl.CostEstimate(flops=int(flops), transcendentals=0, bytes_accessed=0),
    )(*args)


def taps_sent(plan, col):
    return (2 * col,) if plan.two else (0, 2)


def taps_got(plan, col):
    return (2 - 2 * col,) if plan.two else (0, 2)


def far_rows(plan):
    group = lax.axis_index("row") // (FAR // plan.tile_rows)
    one = 2 - 2 * (group % 2)
    return one, 2 - one


def far_one(plan, a, b, w, stream, part_one, part_two, own_a, own_b, *side_b):
    col = lax.axis_index("col")
    one, two = far_rows(plan)
    half = a.shape[0]
    part_one[...] = times(a[...], w[two, 1])
    part_two[...] = times(a[...], w[one, 1])
    own_a[...] = stream[0:half] + times(a[...], w[1, 1])
    own_b[...] = stream[half : 2 * half] + times(b[...], w[1, 1])
    for ref, tap in zip(side_b, taps_sent(plan, col)):
        ref[...] = times(b[...], w[1, tap])


def far_two(plan, n_side, *refs):
    crossed = refs[:n_side]
    got_one, got_two, w, part_one, part_two = refs[n_side : n_side + 5]
    side_b = refs[n_side + 5 : 2 * n_side + 5]
    out_one, out_two = refs[2 * n_side + 5 : 2 * n_side + 7]
    side_out = refs[2 * n_side + 7 :]
    col = lax.axis_index("col")
    one, two = far_rows(plan)
    for part, out, tap_row in ((part_one, out_one, two), (part_two, out_two, one)):
        total = part[...]
        for ref, tap in zip(crossed, taps_got(plan, col)):
            total = total + times(ref[...], w[tap_row, tap])
        out[...] = total.astype(out.dtype)
    for ref, acc, tap in zip(side_out, side_b, taps_sent(plan, col)):
        ref[...] = (acc[...] + times(got_one[...], w[one, tap]) + times(got_two[...], w[two, tap])).astype(ref.dtype)


def far_three(plan, n_side, *refs):
    crossed = refs[:n_side]
    got_one, got_two, w, own_a, own_b, out_a, out_b = refs[n_side:]
    col = lax.axis_index("col")
    one, two = far_rows(plan)
    total = own_a[...]
    for ref, tap in zip(crossed, taps_got(plan, col)):
        total = total + times(ref[...], w[1, tap])
    out_a[...] = total
    out_b[...] = own_b[...] + times(got_one[...], w[one, 1]) + times(got_two[...], w[two, 1])


def far_four(n_side, own_a, own_b, from_above, from_below, *refs):
    side_b, (out_ref,) = refs[:n_side], refs[n_side:]
    half = own_a.shape[0]
    out_ref[0:half] = own_a[...] + from_above[...].astype(jnp.float32) + from_below[...].astype(jnp.float32)
    total = own_b[...]
    for ref in side_b:
        total = total + ref[...].astype(jnp.float32)
    out_ref[half : 2 * half] = total


def pair(value, hop, parity):
    n_row, n_col = lax.axis_size("row"), lax.axis_size("col")
    ups = [
        (r * n_col + c, (r + hop) * n_col + c)
        for r in range(n_row - hop)
        for c in range(n_col)
        if r // hop % 2 == parity
    ]
    return lax.ppermute(value, ("row", "col"), ups + [(j, i) for i, j in ups])


def move(value, rows, cols):
    n_row, n_col = lax.axis_size("row"), lax.axis_size("col")
    pairs = [
        (r * n_col + c, (r + rows) * n_col + c + cols)
        for r in range(n_row)
        for c in range(n_col)
        if 0 <= r + rows < n_row and 0 <= c + cols < n_col
    ]
    return lax.ppermute(value, ("row", "col"), pairs)


def cross(value):
    return lax.ppermute(value, "col", [(0, 1), (1, 0)])


def local(features, inner_weights, far_weights, gains):
    tile_rows, tile_cols, ch = features.shape
    plan = Plan(tile_rows, tile_cols, ch, lax.axis_size("row"), lax.axis_size("col"))
    col = lax.axis_index("col")
    d_one, d_two, d_three, d_four = DILATIONS
    halo = d_one + d_two
    ext, width, width4 = plan.ext, plan.width, plan.width4
    bf16, f32 = jnp.bfloat16, jnp.float32
    shape, vmem, dma = jax.ShapeDtypeStruct, pltpu.VMEM, pltpu.SemaphoreType.DMA
    weights = inner_weights.reshape(inner_weights.shape[0], 9 * ch, ch)
    if plan.two:
        edge = lax.dynamic_slice_in_dim(features, (1 - col) * (tile_cols - ext), ext, axis=1)
        sides = [cross(edge)]
    else:
        sides = [move(features[:, tile_cols - ext :], 0, 1), move(features[:, :ext], 0, -1)]
    n_side = len(sides)
    halo_shape = shape((halo, width, ch), bf16)
    one, two = call(
        functools.partial(gather_rows, plan, halo),
        (halo_shape, halo_shape),
        [dma((2 * (1 + n_side),))],
        (features, *sides),
        1,
    )
    got_two, got_one = pair(two, 1, 1), pair(one, 1, 0)
    per_row = 2 * 9 * ch * ch
    whole = 9 * ch
    n_mid = tile_rows - 2 * d_two
    line = vmem((tile_rows, width + 2 * PAD, ch), f32)
    taps = vmem((tile_rows, width, 3 * ch), bf16)
    mid, mid_act, edge_act, edge_base = call(
        functools.partial(one_own, plan, halo),
        (
            shape((n_mid, width, ch), f32),
            shape((n_mid, width, ch), bf16),
            shape((2 * halo, width, ch), bf16),
            shape((2 * halo, width, ch), f32),
        ),
        [vmem((tile_rows, width, ch), f32), line, taps, vmem((whole, ch), bf16), dma],
        (features, *sides, weights, gains),
        per_row * n_mid * width,
        any_args=(1 + n_side,),
    )
    sent = shape((d_three, width, ch), bf16)
    stream2, act3, one, two = call(
        functools.partial(one_two, plan, halo),
        (shape((tile_rows, width, ch), f32), shape((tile_rows, width, ch), bf16), sent, sent),
        [
            vmem((4 * halo, width, ch), f32),
            vmem((n_mid + 2 * CHUNK, width + 2 * PAD, ch), f32),
            vmem((4 * halo, width, 3 * ch), bf16),
            vmem((2 * CHUNK, width, ch), f32),
            vmem((n_mid + 2 * CHUNK, width, 3 * ch), bf16),
            vmem((whole, ch), bf16),
            vmem((whole, ch), bf16),
            dma((2,)),
        ],
        (got_one, got_two, mid, mid_act, edge_act, edge_base, weights, gains),
        per_row * (2 * CHUNK + tile_rows) * width,
        any_args=(6,),
    )
    got_two, got_one = pair(two, 1, 1), pair(one, 1, 0)
    n_mid = tile_rows - 2 * d_three
    row_f32 = vmem((tile_rows, width, ch), f32)
    edge, mid, mid_act = call(
        functools.partial(three_own, plan),
        (
            shape((2 * d_three, width, ch), f32),
            shape((n_mid, tile_cols, ch), f32),
            shape((n_mid, width4, ch), bf16),
        ),
        [line, taps, row_f32, row_f32, vmem((whole, ch), bf16), dma],
        (act3, weights, stream2, gains),
        per_row * tile_rows * width,
        any_args=(1,),
    )
    sent = shape((d_four, width4, ch), bf16)
    stream3, act4, one, two = call(
        functools.partial(three_rim, plan),
        (shape((tile_rows, tile_cols, ch), f32), shape((tile_rows, width4, ch), bf16), sent, sent),
        [
            vmem((2 * d_three, width + 2 * PAD, ch), f32),
            vmem((2 * d_three, width, 3 * ch), bf16),
            vmem((2, 3 * ch, ch), bf16),
            vmem((2 * d_three, width, ch), f32),
            vmem((2 * d_three, width, ch), f32),
            dma((2,)),
        ],
        (got_one, got_two, edge, mid, mid_act, weights, gains),
        per_row * 2 * d_three * width / 3,
        any_args=(5,),
    )
    got_two, got_one = pair(two, 1, 1), pair(one, 1, 0)
    line = vmem((tile_rows, width4 + 2 * PAD, ch), f32)
    taps = vmem((tile_rows, tile_cols, 3 * ch), bf16)
    acc4 = call(
        functools.partial(four_own, plan),
        shape((tile_rows, tile_cols, ch), f32),
        [line, taps, vmem((whole, ch), bf16), dma],
        (act4, weights, stream3),
        per_row * tile_rows * tile_cols,
        any_args=(1,),
    )
    half = tile_rows // 2
    stream4, a, b = call(
        functools.partial(four_rim, plan),
        (
            shape((tile_rows, tile_cols, ch), f32),
            shape((half, tile_cols, ch), bf16),
            shape((half, tile_cols, ch), bf16),
        ),
        [line, taps, vmem((2, 3 * ch, ch), bf16), dma((2,))],
        (got_one, got_two, acc4, weights, gains),
        per_row * 2 * d_four * tile_cols / 3,
        any_args=(3,),
    )
    row_hop, col_hop = FAR // tile_rows, FAR // tile_cols
    if plan.two:
        crossed = [cross(a)]
    else:
        crossed = [move(a, 0, col_hop), move(a, 0, -col_hop)]
    got_one, got_two = pair(b, row_hop, 0), pair(b, row_hop, 1)
    block = shape((half, tile_cols, ch), f32)
    sent = shape((half, tile_cols, ch), bf16)
    per_half = 2 * ch * ch * half * tile_cols
    part_one, part_two, own_a, own_b, *side_b = call(
        functools.partial(far_one, plan),
        [block] * (4 + n_side),
        [],
        (a, b, far_weights, stream4),
        per_half * 5,
    )
    one, two, *sides = call(
        functools.partial(far_two, plan, n_side),
        [sent] * (2 + n_side),
        [],
        (*crossed, got_one, got_two, far_weights, part_one, part_two, *side_b),
        per_half * 4,
    )
    back_one, back_two = pair(one, row_hop, 0), pair(two, row_hop, 1)
    if plan.two:
        side_got = [cross(sides[0])]
    else:
        side_got = [move(sides[0], 0, col_hop), move(sides[1], 0, -col_hop)]
    own_a, own_b = call(
        functools.partial(far_three, plan, n_side),
        [block] * 2,
        [],
        (*crossed, got_one, got_two, far_weights, own_a, own_b),
        per_half * 3,
    )
    return call(
        functools.partial(far_four, n_side),
        shape((tile_rows, tile_cols, ch), f32),
        [],
        (own_a, own_b, back_one, back_two, *side_got),
        1,
    )


def solution(mesh):
    return jax.shard_map(
        local,
        mesh=mesh,
        in_specs=(P("row", "col", None), P(), P(), P()),
        out_specs=P("row", "col", None),
        check_vma=False,
    )
```

profile of v0, /device:TPU:9, one launch (start us, length us, event | category | flops | bytes accessed | tf_op | source)
XLA Modules:
  0.0 91.4 jit_solution(5235402699396271005)
XLA Ops:
  0.0 0.9 %constant_dynamic-slice_fusion = bf16[16,16,384]{2,1,0:T(8,128)(2,1)S(1)} fusion(bf16[16,64,384]{2,1,0:T(8,128)(2,1)} %refs_0_.1, s32[]{:T(128)S(6)} %select_n.3), kind=kLoop, calls=%fused_computation | loop fusion | bytes 393220 | tf_op jit(solution)/shard_map/dynamic_slice | solution.py:479
  1.0 1.3 %collective-permute-start = (bf16[16,16,384]{2,1,0:T(8,128)(2,1)S(1)}, bf16[16,16,384]{2,1,0:T(8,128)(2,1)S(1)}, u32[]{:S(2)}, u32[]{:S(2)}) collective-permute-start(bf16[16,16,384]{2,1,0:T(8,128)(2,1)S(1)} %constant_dynamic-slice_fusion), channel_id=1, source_target_pairs={{0,1},{1,0},{2,3},{3,2},{4,5},{5,4},{6,7},{7,6},{8,9},{9,8},{10,11... | collective-permute-start | bytes 589832 | tf_op jit(solution)/shard_map/ppermute | solution.py:465
  2.2 4.6 %collective-permute-done.refs_0_.refs_1_ = bf16[16,16,384]{2,1,0:T(8,128)(2,1)S(1)} collective-permute-done((bf16[16,16,384]{2,1,0:T(8,128)(2,1)S(1)}, bf16[16,16,384]{2,1,0:T(8,128)(2,1)S(1)}, u32[]{:S(2)}, u32[]{:S(2)}) %collective-permute-start) | collective-permute-done | bytes 196640 | tf_op jit(solution)/shard_map/ppermute | solution.py:465
  6.8 1.1 %copy-done.1 = bf16[16,64,384]{2,1,0:T(8,128)(2,1)S(1)} copy-done((bf16[16,64,384]{2,1,0:T(8,128)(2,1)S(1)}, bf16[16,64,384]{2,1,0:T(8,128)(2,1)}, u32[]{:S(2)}) %copy-start.1) | copy-done | bytes 786456
  8.1 1.6 %collective-permute-start.1 = (bf16[3,80,384]{2,1,0:T(8,128)(2,1)S(1)}, bf16[3,80,384]{2,1,0:T(8,128)(2,1)S(1)}, u32[]{:S(2)}, u32[]{:S(2)}) collective-permute-start(bf16[3,80,384]{2,1,0:T(8,128)(2,1)S(1)} %get-tuple-element.35), channel_id=1, source_target_pairs={{0,2},{1,3},{4,6},{5,7},{8,10},{9,11},{12,14},{13,15},{16,18},{17,... | collective-permute-start | bytes 552968 | tf_op jit(solution)/shard_map/ppermute | solution.py:450
  9.7 3.0 %collective-permute-start.2 = (bf16[3,80,384]{2,1,0:T(8,128)(2,1)S(1)}, bf16[3,80,384]{2,1,0:T(8,128)(2,1)S(1)}, u32[]{:S(2)}, u32[]{:S(2)}) collective-permute-start(bf16[3,80,384]{2,1,0:T(8,128)(2,1)S(1)} %get-tuple-element.36), channel_id=1, source_target_pairs={{2,4},{3,5},{6,8},{7,9},{10,12},{11,13},{14,16},{15,17},{18,20},{1... | collective-permute-start | bytes 552968 | tf_op jit(solution)/shard_map/ppermute | solution.py:450
  12.8 0.7 copy-done.2
  13.5 6.3 %shard_map.47 = (f32[12,80,384]{2,1,0:T(8,128)S(1)}, bf16[12,80,384]{2,1,0:T(8,128)(2,1)S(1)}, bf16[6,80,384]{2,1,0:T(8,128)(2,1)S(1)}, f32[6,80,384]{2,1,0:T(8,128)S(1)}) custom-call(bf16[16,64,384]{2,1,0:T(8,128)(2,1)S(1)} %copy-done.1, bf16[16,16,384]{2,1,0:T(8,128)(2,1)S(1)} %collective-permute-done.refs_0_.refs_1_, bf16[4,3456,384]{2,1,0:T(8,128)(2,1)} %bitcast.1, ...), custom_call_target="tpu_custom_call" | custom-call | flops 2548039680 | tf_op jit(solution)/shard_map/pallas_call | solution.py:363
  19.9 10.2 %shard_map.48 = (f32[16,80,384]{2,1,0:T(8,128)S(1)}, bf16[16,80,384]{2,1,0:T(8,128)(2,1)S(1)}, bf16[4,80,384]{2,1,0:T(8,128)(2,1)S(1)}, bf16[4,80,384]{2,1,0:T(8,128)(2,1)S(1)}) custom-call(bf16[3,80,384]{2,1,0:T(8,128)(2,1)S(1)} %collective-permute-done.1.refs_0_, bf16[3,80,384]{2,1,0:T(8,128)(2,1)S(1)} %collective-permute-done.2.refs_1_, ...), custom_call_target="tpu_custom_call" | custom-call | flops 5096079360 | tf_op jit(solution)/shard_map/pallas_call | solution.py:363
  30.1 0.5 collective-permute-start.3
  30.5 3.1 %collective-permute-start.4 = (bf16[4,80,384]{2,1,0:T(8,128)(2,1)S(1)}, bf16[4,80,384]{2,1,0:T(8,128)(2,1)S(1)}, u32[]{:S(2)}, u32[]{:S(2)}) collective-permute-start(bf16[4,80,384]{2,1,0:T(8,128)(2,1)S(1)} %get-tuple-element.42), channel_id=1, source_target_pairs={{2,4},{3,5},{6,8},{7,9},{10,12},{11,13},{14,16},{15,17},{18,20},{1... | collective-permute-start | bytes 737288 | tf_op jit(solution)/shard_map/ppermute | solution.py:450
  33.7 6.4 %shard_map.49 = (f32[8,80,384]{2,1,0:T(8,128)S(1)}, f32[8,64,384]{2,1,0:T(8,128)S(1)}, bf16[8,72,384]{2,1,0:T(8,128)(2,1)S(1)}) custom-call(bf16[16,80,384]{2,1,0:T(8,128)(2,1)S(1)} %get-tuple-element.43.act, bf16[4,3456,384]{2,1,0:T(8,128)(2,1)} %bitcast.3, f32[16,80,384]{2,1,0:T(8,128)S(1)} %get-tuple-element.44.stream, f32[5,384]{1,0:T(8,128)S(1)} %copy-done.3), custom_call_target="tpu_custom_call" | custom-call | flops 3397386240 | tf_op jit(solution)/shard_map/pallas_call | solution.py:363
  40.1 0.6 collective-permute-done.4.got_two
  40.7 3.1 %shard_map.50 = (f32[16,64,384]{2,1,0:T(8,128)S(1)}, bf16[16,72,384]{2,1,0:T(8,128)(2,1)S(1)}, bf16[8,72,384]{2,1,0:T(8,128)(2,1)S(1)}, bf16[8,72,384]{2,1,0:T(8,128)(2,1)S(1)}) custom-call(bf16[4,80,384]{2,1,0:T(8,128)(2,1)S(1)} %collective-permute-done.3.got_one, bf16[4,80,384]{2,1,0:T(8,128)(2,1)S(1)} %collective-permute-done.4.got_two, ...), custom_call_target="tpu_custom_call" | custom-call | flops 566231040 | tf_op jit(solution)/shard_map/pallas_call | solution.py:363
  43.8 3.2 %collective-permute-start.6 = (bf16[8,72,384]{2,1,0:T(8,128)(2,1)S(1)}, bf16[8,72,384]{2,1,0:T(8,128)(2,1)S(1)}, u32[]{:S(2)}, u32[]{:S(2)}) collective-permute-start(bf16[8,72,384]{2,1,0:T(8,128)(2,1)S(1)} %get-tuple-element.49), channel_id=1, source_target_pairs={{2,4},{3,5},{6,8},{7,9},{10,12},{11,13},{14,16},{15,17},{18,20},{1... | collective-permute-start | bytes 1327112 | tf_op jit(solution)/shard_map/ppermute | solution.py:450
  47.0 4.4 %shard_map.51.acc = f32[16,64,384]{2,1,0:T(8,128)S(1)} custom-call(bf16[16,72,384]{2,1,0:T(8,128)(2,1)S(1)} %get-tuple-element.50.act, bf16[4,3456,384]{2,1,0:T(8,128)(2,1)} %bitcast.5, f32[16,64,384]{2,1,0:T(8,128)S(1)} %get-tuple-element.51.stream), custom_call_target="tpu_custom_call" | custom-call | flops 2717908992 | tf_op jit(solution)/shard_map/pallas_call | solution.py:363
  51.4 6.8 %collective-permute-done.6.got_two = bf16[8,72,384]{2,1,0:T(8,128)(2,1)S(1)} collective-permute-done((bf16[8,72,384]{2,1,0:T(8,128)(2,1)S(1)}, bf16[8,72,384]{2,1,0:T(8,128)(2,1)S(1)}, u32[]{:S(2)}, u32[]{:S(2)}) %collective-permute-start.6) | collective-permute-done | bytes 442400 | tf_op jit(solution)/shard_map/ppermute | solution.py:450
  58.2 4.3 %shard_map.52 = (f32[16,64,384]{2,1,0:T(8,128)S(1)}, bf16[8,64,384]{2,1,0:T(8,128)(2,1)S(1)}, bf16[8,64,384]{2,1,0:T(8,128)(2,1)S(1)}) custom-call(bf16[8,72,384]{2,1,0:T(8,128)(2,1)S(1)} %collective-permute-done.5.got_one, bf16[8,72,384]{2,1,0:T(8,128)(2,1)S(1)} %collective-permute-done.6.got_two, f32[16,64,384]{2,1,0:T(8,128)S(1)} %shard_map.51.acc, ...), custom_call_target="tpu_custom_call" | custom-call | flops 905969664 | tf_op jit(solution)/shard_map/pallas_call | solution.py:363
  62.5 1.3 %collective-permute-start.7 = (bf16[8,64,384]{2,1,0:T(8,128)(2,1)S(1)}, bf16[8,64,384]{2,1,0:T(8,128)(2,1)S(1)}, u32[]{:S(2)}, u32[]{:S(2)}) collective-permute-start(bf16[8,64,384]{2,1,0:T(8,128)(2,1)S(1)} %get-tuple-element.52.a), channel_id=1, source_target_pairs={{0,1},{1,0},{2,3},{3,2},{4,5},{5,4},{6,7},{7,6},{8,9},{9,8},{10,11... | collective-permute-start | bytes 1179656 | tf_op jit(solution)/shard_map/ppermute | solution.py:465
  63.8 4.7 %collective-permute-start.9 = (bf16[8,64,384]{2,1,0:T(8,128)(2,1)S(1)}, bf16[8,64,384]{2,1,0:T(8,128)(2,1)S(1)}, u32[]{:S(2)}, u32[]{:S(2)}) collective-permute-start(bf16[8,64,384]{2,1,0:T(8,128)(2,1)S(1)} %get-tuple-element.53.b), channel_id=1, source_target_pairs={{8,16},{9,17},{10,18},{11,19},{12,20},{13,21},{14,22},{15,23},{16,... | collective-permute-start | bytes 1179656 | tf_op jit(solution)/shard_map/ppermute | solution.py:450
  68.6 1.4 %shard_map.53 = (f32[8,64,384]{2,1,0:T(8,128)S(1)}, f32[8,64,384]{2,1,0:T(8,128)S(1)}, f32[8,64,384]{2,1,0:T(8,128)S(1)}, f32[8,64,384]{2,1,0:T(8,128)S(1)}, f32[8,64,384]{2,1,0:T(8,128)S(1)}) custom-call(bf16[8,64,384]{2,1,0:T(8,128)(2,1)S(1)} %get-tuple-element.52.a, bf16[8,64,384]{2,1,0:T(8,128)(2,1)S(1)} %get-tuple-element.53.b, ...), custom_call_target="tpu_custom_call" | custom-call | flops 754974720 | tf_op jit(solution)/shard_map/pallas_call | solution.py:363
  70.0 1.0 %collective-permute-done.7.refs_0_ = bf16[8,64,384]{2,1,0:T(8,128)(2,1)S(1)} collective-permute-done((bf16[8,64,384]{2,1,0:T(8,128)(2,1)S(1)}, bf16[8,64,384]{2,1,0:T(8,128)(2,1)S(1)}, u32[]{:S(2)}, u32[]{:S(2)}) %collective-permute-start.7) | collective-permute-done | bytes 393248 | tf_op jit(solution)/shard_map/ppermute | solution.py:465
  70.9 1.5 %collective-permute-done.8.refs_1_ = bf16[8,64,384]{2,1,0:T(8,128)(2,1)S(1)} collective-permute-done((bf16[8,64,384]{2,1,0:T(8,128)(2,1)S(1)}, bf16[8,64,384]{2,1,0:T(8,128)(2,1)S(1)}, u32[]{:S(2)}, u32[]{:S(2)}) %collective-permute-start.8) | collective-permute-done | bytes 393248 | tf_op jit(solution)/shard_map/ppermute | solution.py:450
  72.5 2.7 %collective-permute-done.9.refs_2_ = bf16[8,64,384]{2,1,0:T(8,128)(2,1)S(1)} collective-permute-done((bf16[8,64,384]{2,1,0:T(8,128)(2,1)S(1)}, bf16[8,64,384]{2,1,0:T(8,128)(2,1)S(1)}, u32[]{:S(2)}, u32[]{:S(2)}) %collective-permute-start.9) | collective-permute-done | bytes 393248 | tf_op jit(solution)/shard_map/ppermute | solution.py:450
  75.2 1.1 %shard_map.55 = (bf16[8,64,384]{2,1,0:T(8,128)(2,1)S(1)}, bf16[8,64,384]{2,1,0:T(8,128)(2,1)S(1)}, bf16[8,64,384]{2,1,0:T(8,128)(2,1)S(1)}) custom-call(bf16[8,64,384]{2,1,0:T(8,128)(2,1)S(1)} %collective-permute-done.7.refs_0_, bf16[8,64,384]{2,1,0:T(8,128)(2,1)S(1)} %collective-permute-done.8.refs_1_, ...), custom_call_target="tpu_custom_call" | custom-call | flops 603979776 | tf_op jit(solution)/shard_map/pallas_call | solution.py:363
  76.4 3.6 %collective-permute-start.11 = (bf16[8,64,384]{2,1,0:T(8,128)(2,1)S(1)}, bf16[8,64,384]{2,1,0:T(8,128)(2,1)S(1)}, u32[]{:S(2)}, u32[]{:S(2)}) collective-permute-start(bf16[8,64,384]{2,1,0:T(8,128)(2,1)S(1)} %get-tuple-element.63), channel_id=1, source_target_pairs={{8,16},{9,17},{10,18},{11,19},{12,20},{13,21},{14,22},{15,23},{16,... | collective-permute-start | bytes 1179656 | tf_op jit(solution)/shard_map/ppermute | solution.py:450
  80.0 0.3 collective-permute-start.12
  80.3 0.9 shard_map.54
  81.2 4.9 %collective-permute-done.10.from_above = bf16[8,64,384]{2,1,0:T(8,128)(2,1)S(1)} collective-permute-done((bf16[8,64,384]{2,1,0:T(8,128)(2,1)S(1)}, bf16[8,64,384]{2,1,0:T(8,128)(2,1)S(1)}, u32[]{:S(2)}, u32[]{:S(2)}) %collective-permute-start.10) | collective-permute-done | bytes 393248 | tf_op jit(solution)/shard_map/ppermute | solution.py:450
  86.1 2.2 %collective-permute-done.11.from_below = bf16[8,64,384]{2,1,0:T(8,128)(2,1)S(1)} collective-permute-done((bf16[8,64,384]{2,1,0:T(8,128)(2,1)S(1)}, bf16[8,64,384]{2,1,0:T(8,128)(2,1)S(1)}, u32[]{:S(2)}, u32[]{:S(2)}) %collective-permute-start.11) | collective-permute-done | bytes 393248 | tf_op jit(solution)/shard_map/ppermute | solution.py:450
  88.3 1.8 %collective-permute-done.12.refs_0_ = bf16[8,64,384]{2,1,0:T(8,128)(2,1)S(1)} collective-permute-done((bf16[8,64,384]{2,1,0:T(8,128)(2,1)S(1)}, bf16[8,64,384]{2,1,0:T(8,128)(2,1)S(1)}, u32[]{:S(2)}, u32[]{:S(2)}) %collective-permute-start.12) | collective-permute-done | bytes 393248 | tf_op jit(solution)/shard_map/ppermute | solution.py:465
  90.1 1.3 %shard_map.56 = f32[16,64,384]{2,1,0:T(8,128)} custom-call(f32[8,64,384]{2,1,0:T(8,128)S(1)} %get-tuple-element.57.own_a, f32[8,64,384]{2,1,0:T(8,128)S(1)} %get-tuple-element.58.own_b, bf16[8,64,384]{2,1,0:T(8,128)(2,1)S(1)} %collective-permute-done.10.from_above, bf16[8,64,384]{2,1,0:T(8,128)(2,1)S(1)} %collective-permute-done.11.from_below, ...), custom_call_target="tpu_custom_call" | custom-call | flops 1 | tf_op jit(solution)/shard_map/pallas_call | solution.py:363
  (14 shorter events, 0.4 us)
Async XLA Ops:
  1.0 5.9 %collective-permute-start = (bf16[16,16,384]{2,1,0:T(8,128)(2,1)S(1)}, bf16[16,16,384]{2,1,0:T(8,128)(2,1)S(1)}, u32[]{:S(2)}, u32[]{:S(2)}) collective-permute-start(bf16[16,16,384]{2,1,0:T(8,128)(2,1)S(1)} %constant_dynamic-slice_fusion), channel_id=1, source_target_pairs={{0,1},{1,0},{2,3},{3,2},{4,5},{5,4},{6,7},{7,6},{8,9},{9,8},{10,11... | collective-permute-start | bytes 589832 | tf_op jit(solution)/shard_map/ppermute | solution.py:465
  6.8 1.1 %copy-start.1 = (bf16[16,64,384]{2,1,0:T(8,128)(2,1)S(1)}, bf16[16,64,384]{2,1,0:T(8,128)(2,1)}, u32[]{:S(2)}) copy-start(bf16[16,64,384]{2,1,0:T(8,128)(2,1)} %refs_0_.1) | copy-start | bytes 2359300
  8.1 11.7 %collective-permute-start.1 = (bf16[3,80,384]{2,1,0:T(8,128)(2,1)S(1)}, bf16[3,80,384]{2,1,0:T(8,128)(2,1)S(1)}, u32[]{:S(2)}, u32[]{:S(2)}) collective-permute-start(bf16[3,80,384]{2,1,0:T(8,128)(2,1)S(1)} %get-tuple-element.35), channel_id=1, source_target_pairs={{0,2},{1,3},{4,6},{5,7},{8,10},{9,11},{12,14},{13,15},{16,18},{17,... | collective-permute-start | bytes 552968 | tf_op jit(solution)/shard_map/ppermute | solution.py:450
  9.7 10.1 %collective-permute-start.2 = (bf16[3,80,384]{2,1,0:T(8,128)(2,1)S(1)}, bf16[3,80,384]{2,1,0:T(8,128)(2,1)S(1)}, u32[]{:S(2)}, u32[]{:S(2)}) collective-permute-start(bf16[3,80,384]{2,1,0:T(8,128)(2,1)S(1)} %get-tuple-element.36), channel_id=1, source_target_pairs={{2,4},{3,5},{6,8},{7,9},{10,12},{11,13},{14,16},{15,17},{18,20},{1... | collective-permute-start | bytes 552968 | tf_op jit(solution)/shard_map/ppermute | solution.py:450
  12.8 0.7 copy-start.2
  13.5 6.4 %copy-start.3 = (f32[5,384]{1,0:T(8,128)S(1)}, f32[5,384]{1,0:T(8,128)}, u32[]{:S(2)}) copy-start(f32[5,384]{1,0:T(8,128)} %gains.5) | copy-start | bytes 23044
  30.1 10.0 %collective-permute-start.3 = (bf16[4,80,384]{2,1,0:T(8,128)(2,1)S(1)}, bf16[4,80,384]{2,1,0:T(8,128)(2,1)S(1)}, u32[]{:S(2)}, u32[]{:S(2)}) collective-permute-start(bf16[4,80,384]{2,1,0:T(8,128)(2,1)S(1)} %get-tuple-element.41), channel_id=1, source_target_pairs={{0,2},{1,3},{4,6},{5,7},{8,10},{9,11},{12,14},{13,15},{16,18},{17,... | collective-permute-start | bytes 737288 | tf_op jit(solution)/shard_map/ppermute | solution.py:450
  30.5 10.1 %collective-permute-start.4 = (bf16[4,80,384]{2,1,0:T(8,128)(2,1)S(1)}, bf16[4,80,384]{2,1,0:T(8,128)(2,1)S(1)}, u32[]{:S(2)}, u32[]{:S(2)}) collective-permute-start(bf16[4,80,384]{2,1,0:T(8,128)(2,1)S(1)} %get-tuple-element.42), channel_id=1, source_target_pairs={{2,4},{3,5},{6,8},{7,9},{10,12},{11,13},{14,16},{15,17},{18,20},{1... | collective-permute-start | bytes 737288 | tf_op jit(solution)/shard_map/ppermute | solution.py:450
  43.7 7.7 %collective-permute-start.5 = (bf16[8,72,384]{2,1,0:T(8,128)(2,1)S(1)}, bf16[8,72,384]{2,1,0:T(8,128)(2,1)S(1)}, u32[]{:S(2)}, u32[]{:S(2)}) collective-permute-start(bf16[8,72,384]{2,1,0:T(8,128)(2,1)S(1)} %get-tuple-element.48), channel_id=1, source_target_pairs={{0,2},{1,3},{4,6},{5,7},{8,10},{9,11},{12,14},{13,15},{16,18},{17,... | collective-permute-start | bytes 1327112 | tf_op jit(solution)/shard_map/ppermute | solution.py:450
  43.8 14.4 %collective-permute-start.6 = (bf16[8,72,384]{2,1,0:T(8,128)(2,1)S(1)}, bf16[8,72,384]{2,1,0:T(8,128)(2,1)S(1)}, u32[]{:S(2)}, u32[]{:S(2)}) collective-permute-start(bf16[8,72,384]{2,1,0:T(8,128)(2,1)S(1)} %get-tuple-element.49), channel_id=1, source_target_pairs={{2,4},{3,5},{6,8},{7,9},{10,12},{11,13},{14,16},{15,17},{18,20},{1... | collective-permute-start | bytes 1327112 | tf_op jit(solution)/shard_map/ppermute | solution.py:450
  58.2 10.4 %copy-start = (bf16[3,3,384,384]{3,2,1,0:T(8,128)(2,1)S(1)}, bf16[3,3,384,384]{3,2,1,0:T(8,128)(2,1)}, u32[]{:S(2)}) copy-start(bf16[3,3,384,384]{3,2,1,0:T(8,128)(2,1)} %refs_3_.5) | copy-start | bytes 7962628
  62.5 8.4 %collective-permute-start.7 = (bf16[8,64,384]{2,1,0:T(8,128)(2,1)S(1)}, bf16[8,64,384]{2,1,0:T(8,128)(2,1)S(1)}, u32[]{:S(2)}, u32[]{:S(2)}) collective-permute-start(bf16[8,64,384]{2,1,0:T(8,128)(2,1)S(1)} %get-tuple-element.52.a), channel_id=1, source_target_pairs={{0,1},{1,0},{2,3},{3,2},{4,5},{5,4},{6,7},{7,6},{8,9},{9,8},{10,11... | collective-permute-start | bytes 1179656 | tf_op jit(solution)/shard_map/ppermute | solution.py:465
  63.8 8.6 %collective-permute-start.8 = (bf16[8,64,384]{2,1,0:T(8,128)(2,1)S(1)}, bf16[8,64,384]{2,1,0:T(8,128)(2,1)S(1)}, u32[]{:S(2)}, u32[]{:S(2)}) collective-permute-start(bf16[8,64,384]{2,1,0:T(8,128)(2,1)S(1)} %get-tuple-element.53.b), channel_id=1, source_target_pairs={{0,8},{1,9},{2,10},{3,11},{4,12},{5,13},{6,14},{7,15},{16,24},{17,... | collective-permute-start | bytes 1179656 | tf_op jit(solution)/shard_map/ppermute | solution.py:450
  63.8 11.3 %collective-permute-start.9 = (bf16[8,64,384]{2,1,0:T(8,128)(2,1)S(1)}, bf16[8,64,384]{2,1,0:T(8,128)(2,1)S(1)}, u32[]{:S(2)}, u32[]{:S(2)}) collective-permute-start(bf16[8,64,384]{2,1,0:T(8,128)(2,1)S(1)} %get-tuple-element.53.b), channel_id=1, source_target_pairs={{8,16},{9,17},{10,18},{11,19},{12,20},{13,21},{14,22},{15,23},{16,... | collective-permute-start | bytes 1179656 | tf_op jit(solution)/shard_map/ppermute | solution.py:450
  76.3 9.8 %collective-permute-start.10 = (bf16[8,64,384]{2,1,0:T(8,128)(2,1)S(1)}, bf16[8,64,384]{2,1,0:T(8,128)(2,1)S(1)}, u32[]{:S(2)}, u32[]{:S(2)}) collective-permute-start(bf16[8,64,384]{2,1,0:T(8,128)(2,1)S(1)} %get-tuple-element.62), channel_id=1, source_target_pairs={{0,8},{1,9},{2,10},{3,11},{4,12},{5,13},{6,14},{7,15},{16,24},{17,... | collective-permute-start | bytes 1179656 | tf_op jit(solution)/shard_map/ppermute | solution.py:450
  76.4 11.9 %collective-permute-start.11 = (bf16[8,64,384]{2,1,0:T(8,128)(2,1)S(1)}, bf16[8,64,384]{2,1,0:T(8,128)(2,1)S(1)}, u32[]{:S(2)}, u32[]{:S(2)}) collective-permute-start(bf16[8,64,384]{2,1,0:T(8,128)(2,1)S(1)} %get-tuple-element.63), channel_id=1, source_target_pairs={{8,16},{9,17},{10,18},{11,19},{12,20},{13,21},{14,22},{15,23},{16,... | collective-permute-start | bytes 1179656 | tf_op jit(solution)/shard_map/ppermute | solution.py:450
  80.0 10.1 %collective-permute-start.12 = (bf16[8,64,384]{2,1,0:T(8,128)(2,1)S(1)}, bf16[8,64,384]{2,1,0:T(8,128)(2,1)S(1)}, u32[]{:S(2)}, u32[]{:S(2)}) collective-permute-start(bf16[8,64,384]{2,1,0:T(8,128)(2,1)S(1)} %get-tuple-element.64), channel_id=1, source_target_pairs={{0,1},{1,0},{2,3},{3,2},{4,5},{5,4},{6,7},{7,6},{8,9},{9,8},{10,11... | collective-permute-start | bytes 1179656 | tf_op jit(solution)/shard_map/ppermute | solution.py:465
where the time goes:
time: 91.9 us; the launch traced here: 91.4 us
  Pallas kernels  39.6 us (43%)
  waiting for transfers between devices  26.1 us (28%)
  starting transfers between devices  22.8 us (25%)
  local copies, waits for them, and re-layouts  2.79 us (3%)
    pallas_call x11, Pallas kernels, call(): pl.pallas_call(kernel, out_shape=out_shape, in_specs=[pl.BlockSpec(memory...  39.6 us
    ppermute x10, starting transfers between devices, pair(): return lax.ppermute(value, ('row', 'col'), ups + [(j, i) for i, j in ups])  19.9 us
    ppermute x10, waiting for transfers between devices, pair(): return lax.ppermute(value, ('row', 'col'), ups + [(j, i) for i, j in ups])  18.7 us
    ppermute x3, waiting for transfers between devices, cross(): return lax.ppermute(value, 'col', [(0, 1), (1, 0)])  7.36 us
    ppermute x3, starting transfers between devices, cross(): return lax.ppermute(value, 'col', [(0, 1), (1, 0)])  2.86 us
    unnamed x8, local copies, waits for them, and re-layouts  1.84 us
  transfers between devices with their start and end apart: 13, of which 9 were waited for; matrix products, arithmetic and copies ran while one was open for 0% of the time, Pallas kernels for 21%

commit v1 on v0

--- a/solution.py
+++ b/solution.py
@@ -10,7 +10,7 @@
 FAR = 64
 DILATIONS = (1, 2, 4, 8)
 PAD = 8
-VMEM_LIMIT = 40 * 1024 * 1024
+VMEM_LIMIT = 20 * 1024 * 1024
 
 
 def normed(stream, gain):
@@ -74,6 +74,11 @@
             return (pl.multiple_of((1 - col) * self.tile_cols, 8),)
         return (0, self.ext + self.tile_cols)
 
+    def edges(self, col):
+        if self.two:
+            return (pl.multiple_of((1 - col) * (self.tile_cols - self.ext), 16),)
+        return self.tile_cols - self.ext, 0
+
     def col_range(self, col):
         if self.two:
             return 0, self.width
@@ -109,18 +114,32 @@
         body(row)
 
 
-def gather_rows(plan, halo, features, *refs):
+def stage(plan, halo, features, gains, *refs):
     n_side = 1 if plan.two else 2
-    sides, outs, (sems,) = refs[:n_side], refs[n_side : n_side + 2], refs[n_side + 2 :]
+    tile, gains_out = refs[:2]
+    edges, outs, (sems,) = refs[2 : 2 + n_side], refs[2 + n_side : 4 + n_side], refs[4 + n_side :]
     row_id, col = lax.axis_index("row"), lax.axis_index("col")
+    moves = [(features.at[:, pl.ds(at, plan.ext)], edge) for at, edge in zip(plan.edges(col), edges)]
+    moves += [(features.at[pl.ds(at, halo)], out) for at, out in zip(plan.starts(row_id, halo), outs)]
+    moves += [(gains, gains_out), (features, tile)]
+    copies = [pltpu.make_async_copy(src, dst, sems.at[k]) for k, (src, dst) in enumerate(moves)]
+    for copy in copies:
+        copy.start()
+    for copy in copies:
+        copy.wait()
+
+
+def corners(plan, one, two, after, *refs):
+    del after
+    outs, (sems,) = refs[:-1], refs[-1:]
+    col = lax.axis_index("col")
+    halo = one.shape[0]
     copies = []
-    for out, start in zip(outs, plan.starts(row_id, halo)):
-        for part, offset in zip((features,) + sides, (plan.own(col),) + plan.sides(col)):
+    for out, at in zip(outs, plan.edges(col)):
+        for k, ref in enumerate((one, two)):
             copies.append(
                 pltpu.make_async_copy(
-                    part.at[pl.ds(start, halo)],
-                    out.at[:, pl.ds(offset, part.shape[1])],
-                    sems.at[len(copies)],
+                    ref.at[:, pl.ds(at, plan.ext)], out.at[pl.ds(k * halo, halo)], sems.at[len(copies)]
                 )
             )
     for copy in copies:
@@ -132,63 +151,72 @@
 CHUNK = 4
 
 
-def one_own(plan, halo, *refs):
+def one_prepare(plan, halo, *refs):
     n_side = 1 if plan.two else 2
     parts = refs[: 1 + n_side]
-    w_hbm, gains, mid, mid_act, edge_act, edge_base, base, line, taps, weight, sem = refs[1 + n_side :]
-    col = lax.axis_index("col")
-    copy = pltpu.make_async_copy(w_hbm.at[0], weight, sem)
+    gains, w_hbm, base, taps, w_one, line, sem = refs[1 + n_side :]
+    copy = fetch(w_hbm, 0, w_one, sem)
     copy.start()
-    rows, width = plan.tile_rows, plan.width
+    col = lax.axis_index("col")
     for part, offset in zip(parts, (plan.own(col),) + plan.sides(col)):
         base[:, pl.ds(offset, part.shape[1]), :] = part[...].astype(jnp.float32)
     clear_edges(line)
 
     def prepare(row):
-        lay(line, taps, row, plan.inside(col, normed(base[row], gains[0:1, :])), DILATIONS[0], PAD, width)
+        lay(line, taps, row, plan.inside(col, normed(base[row], gains[0:1, :])), DILATIONS[0], PAD, plan.width)
+
+    rows_of(plan.tile_rows, prepare)
+    copy.wait()
+
+
+def fetch(w_hbm, layer, out, sem):
+    return pltpu.make_async_copy(w_hbm.at[layer], out, sem)
+
+
+def one_own(plan, halo, base, taps, w_one, w_hbm, gains, mid, mid_act, w_next, sem):
+    col = lax.axis_index("col")
+    copy = fetch(w_hbm, 1, w_next, sem)
+    copy.start()
 
     def follow(row):
         mid_act[row] = plan.inside(col, normed(mid[row], gains[1:2, :])).astype(mid_act.dtype)
 
-    lead = 2 * CHUNK
-    rows_of(lead, prepare)
-    copy.wait()
     edge = DILATIONS[1]
     count = mid.shape[0] // CHUNK
     for k in range(count):
         at = k * CHUNK
         mid[at : at + CHUNK] = base[edge + at : edge + at + CHUNK] + conv_part(
-            taps, weight, edge + at - DILATIONS[0], CHUNK, DILATIONS[0]
+            taps, w_one, edge + at - DILATIONS[0], CHUNK, DILATIONS[0]
         )
-        for row in range(lead + at, min(lead + at + CHUNK, rows)):
-            prepare(row)
         if k:
             for row in range(at - CHUNK, at):
                 follow(row)
-    ch = plan.ch
-    for k, first in enumerate((0, rows - halo)):
-        edge_act[k * halo : (k + 1) * halo] = taps[first : first + halo, :, ch : 2 * ch]
-        edge_base[k * halo : (k + 1) * halo] = base[first : first + halo]
     rows_of(CHUNK, lambda row: follow((count - 1) * CHUNK + row))
+    copy.wait()
 
 
 def one_two(plan, halo, *refs):
-    got, refs = refs[:2], refs[2:]
-    mid, mid_act, edge_act, edge_base, w_hbm, gains, stream, act, send_one, send_two = refs[:10]
-    base, line, taps_one, rim, taps_two, w_one, w_two, sems = refs[10:]
+    n_side = 1 if plan.two else 2
+    got, crossed, refs = refs[:2], refs[2 : 2 + n_side], refs[2 + n_side :]
+    mid, mid_act, own_taps, own_base, w_one, w_two, w_hbm, gains = refs[:8]
+    stream, taps_out, send_one, send_two, w_next = refs[8:13]
+    base, line, taps_one, rim, taps_two, sem = refs[13:]
+    line_out = line
     row_id, col = lax.axis_index("row"), lax.axis_index("col")
-    copies = [pltpu.make_async_copy(w_hbm.at[k], w, sems.at[k]) for k, w in enumerate((w_one, w_two))]
-    for copy in copies:
-        copy.start()
+    copy = fetch(w_hbm, 2, w_next, sem)
+    copy.start()
     rows, width, ch = plan.tile_rows, plan.width, plan.ch
     d_one, d_two = DILATIONS[:2]
     clear_edges(line)
-    base[halo : 3 * halo] = edge_base[...]
+    for k, first in enumerate((0, rows - halo)):
+        at = (k + 1) * halo
+        base[at : at + halo] = own_base[first : first + halo]
+        taps_one[at : at + halo] = own_taps[first : first + halo]
     top = (halo * 3) * (1 - row_id % 2)
-    for ref, at in zip(got, (top, 3 * halo - top)):
-        base[pl.ds(at, halo)] = ref[...].astype(jnp.float32)
-    for row in range(2 * halo):
-        lay(line, taps_one, halo + row, edge_act[row].astype(jnp.float32), d_one, PAD, width)
+    for k, (ref, at) in enumerate(zip(got, (top, 3 * halo - top))):
+        base[pl.ds(at, halo), pl.ds(plan.own(col), ref.shape[1]), :] = ref[...].astype(jnp.float32)
+        for side, offset in zip(crossed, plan.sides(col)):
+            base[pl.ds(at, halo), pl.ds(offset, side.shape[1]), :] = side[k * halo : (k + 1) * halo].astype(jnp.float32)
     for row in tuple(range(halo)) + tuple(range(3 * halo, 4 * halo)):
         lay(line, taps_one, row, plan.inside(col, normed(base[row], gains[0:1, :])), d_one, PAD, width)
     n_mid = mid.shape[0]
@@ -196,13 +224,11 @@
     def spread_mid(row):
         lay(line, taps_two, 2 * d_two + row, mid_act[row].astype(jnp.float32), d_two, PAD, width)
 
-    copies[0].wait()
     for k in range(2):
         at = 2 * halo * k
         rim[k * CHUNK : (k + 1) * CHUNK] = base[at + 1 : at + 1 + CHUNK] + conv_part(taps_one, w_one, at, CHUNK, d_one)
         for row in range(k * n_mid // 2, (k + 1) * n_mid // 2):
             spread_mid(row)
-    copies[1].wait()
 
     def spread_rim(row):
         value = plan.inside(col, normed(rim[row], gains[1:2, :]))
@@ -213,7 +239,7 @@
         lay(line, taps_two, row if row < CHUNK else n_mid + row, value, d_two, PAD, width)
 
     def finish(row):
-        act[row] = plan.inside(col, normed(stream[row], gains[2:3, :])).astype(act.dtype)
+        lay(line_out, taps_out, row, plan.inside(col, normed(stream[row], gains[2:3, :])), DILATIONS[2], PAD, width)
 
     def second(first):
         return conv_part(taps_two, w_two, first, CHUNK, d_two)
@@ -240,18 +266,16 @@
     rows_of(CHUNK, finish)
     rows_of(CHUNK, lambda row: finish(last + row))
     for ref, at in zip((send_one, send_two), plan.starts(row_id, DILATIONS[2])):
-        ref[...] = act[pl.ds(at, DILATIONS[2])]
-
-
-def three_own(plan, act, w_hbm, stream, gains, edge, mid, mid_act, line, taps, full, row_act, weight, sem):
-    col = lax.axis_index("col")
-    copy = pltpu.make_async_copy(w_hbm.at[2], weight, sem)
+        ref[...] = taps_out[pl.ds(at, DILATIONS[2]), :, ch : 2 * ch]
+    copy.wait()
+
+
+def three_own(plan, taps, weight, w_hbm, stream, gains, edge, mid, mid_act, w_next, full, row_act, sem):
+    col = lax.axis_index("col")
+    copy = fetch(w_hbm, 3, w_next, sem)
     copy.start()
     d = DILATIONS[2]
-    rows, width = plan.tile_rows, plan.width
-    clear_edges(line)
-    rows_of(rows, lambda row: lay(line, taps, row, act[row].astype(jnp.float32), d, PAD, width))
-    copy.wait()
+    rows = plan.tile_rows
     for first in range(d, rows - d, CHUNK):
         full[first - d : first - d + CHUNK] = stream[first : first + CHUNK] + conv_part(taps, weight, first - d, CHUNK, d)
 
@@ -265,6 +289,7 @@
     edge[d : 2 * d] = stream[rows - d : rows] + conv_part(taps, weight, rows - 2 * d, d, d, (0, 1))
     for row in range(count // 2, count):
         finish(row)
+    copy.wait()
 
 
 def emit(plan, col, full, row_act, row, gain, stream, act, at):
@@ -273,23 +298,15 @@
     stream[at] = full[row, pl.ds(plan.own(col), plan.tile_cols), :]
 
 
-def partner_weights(plan, row_id, w_hbm, layer, weight, sems):
-    depth = weight.shape[1]
+def partner_weight(plan, row_id, k, weight):
+    depth = 3 * plan.ch
     one = jnp.where(row_id % 2 == 0, 2 * depth, 0)
-    return [
-        pltpu.make_async_copy(
-            w_hbm.at[layer, pl.ds(pl.multiple_of(at, 16), depth)], weight.at[k], sems.at[k]
-        )
-        for k, at in enumerate((one, 2 * depth - one))
-    ]
-
-
-def three_rim(plan, got_one, got_two, edge, mid, mid_act, w_hbm, gains, stream, act, send_one, send_two, *scratch):
-    line, taps, weight, full, row_act, sems = scratch
+    return weight.at[pl.ds(pl.multiple_of((one, 2 * depth - one)[k], 128), depth)]
+
+
+def three_rim(plan, got_one, got_two, edge, mid, mid_act, weight, gains, stream, act, send_one, send_two, *scratch):
+    line, taps, full, row_act = scratch
     row_id, col = lax.axis_index("row"), lax.axis_index("col")
-    copies = partner_weights(plan, row_id, w_hbm, 2, weight, sems)
-    for copy in copies:
-        copy.start()
     d = DILATIONS[2]
     rows, width = plan.tile_rows, plan.width
     clear_edges(line)
@@ -301,8 +318,9 @@
     at_one, at_two = plan.starts(row_id, d)
     half = jnp.where(row_id % 2 == 0, d, 0)
     for k, (place, at) in enumerate(((half, at_one), (d - half, at_two))):
-        copies[k].wait()
-        full[k * d : (k + 1) * d] = edge[pl.ds(place, d)] + conv_part(taps, weight.at[k], k * d, d, d, (0,))
+        full[k * d : (k + 1) * d] = edge[pl.ds(place, d)] + conv_part(
+            taps, partner_weight(plan, row_id, k, weight), k * d, d, d, (0,)
+        )
     for k, at in enumerate((at_one, at_two)):
         for row in range(d):
             emit(plan, col, full, row_act, k * d + row, gains[3:4, :], stream, act, at + row)
@@ -310,48 +328,44 @@
         ref[...] = act[pl.ds(at, DILATIONS[3])]
 
 
-def four_own(plan, act, w_hbm, stream, out, line, taps, weight, sem):
-    col = lax.axis_index("col")
-    copy = pltpu.make_async_copy(w_hbm.at[3], weight, sem)
-    copy.start()
+def four_own(plan, act, weight, stream, out, line, taps):
+    col = lax.axis_index("col")
     d = DILATIONS[3]
     rows, cols = plan.tile_rows, plan.tile_cols
     start = PAD + plan.own4(col)
     clear_edges(line)
     rows_of(rows, lambda row: lay(line, taps, row, act[row].astype(jnp.float32), d, start, cols))
-    copy.wait()
     for first in range(0, rows, CHUNK):
         used = tuple(t for t in range(3) if 0 <= first + (t - 1) * d < rows)
         out[first : first + CHUNK] = stream[first : first + CHUNK] + conv_part(taps, weight, first - d, CHUNK, d, used)
 
 
-def four_rim(plan, got_one, got_two, acc, w_hbm, gains, stream, act_a, act_b, line, taps, weight, sems):
+def four_rim(plan, k, got, acc, weight, gains, stream, act, line, taps):
     row_id, col = lax.axis_index("row"), lax.axis_index("col")
-    copies = partner_weights(plan, row_id, w_hbm, 3, weight, sems)
-    for copy in copies:
-        copy.start()
     d = DILATIONS[3]
-    rows, cols = plan.tile_rows, plan.tile_cols
     start = PAD + plan.own4(col)
     clear_edges(line)
-    for k, ref in enumerate((got_one, got_two)):
-        rows_of(d, lambda row, k=k, ref=ref: lay(line, taps, k * d + row, ref[row].astype(jnp.float32), d, start, cols))
-    if rows > 2 * d:
-        stream[d : rows - d] = acc[d : rows - d]
-    pending = []
-    for k, at in enumerate(plan.starts(row_id, d)):
-        copies[k].wait()
-        for step in range(0, d, CHUNK):
-            stream[pl.ds(at + step, CHUNK)] = acc[pl.ds(at + step, CHUNK)] + conv_part(
-                taps, weight.at[k], k * d + step, CHUNK, d, (0,)
-            )
-    half = rows // 2
-    for k, act in enumerate((act_a, act_b)):
-
-        def finish(row, act=act, k=k):
-            act[row] = normed(stream[k * half + row], gains[4:5, :]).astype(act.dtype)
-
-        rows_of(half, finish)
+
+    def spread(row):
+        lay(line, taps, row, got[row].astype(jnp.float32), d, start, plan.tile_cols)
+
+    def finish(row):
+        act[row] = normed(stream[row], gains[4:5, :]).astype(act.dtype)
+
+    for row in range(CHUNK):
+        spread(row)
+    at = plan.starts(row_id, d)[k]
+    for first in range(0, d, CHUNK):
+        stream[first : first + CHUNK] = acc[pl.ds(at + first, CHUNK)] + conv_part(
+            taps, partner_weight(plan, row_id, k, weight), first, CHUNK, d, (0,)
+        )
+        if first:
+            for row in range(first - CHUNK, first):
+                finish(row)
+        for row in range(first + CHUNK, min(first + 2 * CHUNK, d)):
+            spread(row)
+    for row in range(d - CHUNK, d):
+        finish(row)
 
 
 def times(a, w):
@@ -364,7 +378,7 @@
         kernel,
         out_shape=out_shape,
         in_specs=[
-            pl.BlockSpec(memory_space=pl.ANY) if k in any_args else pl.BlockSpec(memory_space=pltpu.VMEM)
+            pl.BlockSpec(memory_space=pltpu.HBM) if k in any_args else pl.BlockSpec(memory_space=pltpu.VMEM)
             for k in range(len(args))
         ],
         out_specs=jax.tree.map(lambda _: pl.BlockSpec(memory_space=pltpu.VMEM), out_shape),
@@ -388,15 +402,17 @@
     return one, 2 - one
 
 
-def far_one(plan, a, b, w, stream, part_one, part_two, own_a, own_b, *side_b):
-    col = lax.axis_index("col")
+def far_a(plan, a, w, stream, part_one, part_two, own):
     one, two = far_rows(plan)
-    half = a.shape[0]
     part_one[...] = times(a[...], w[two, 1])
     part_two[...] = times(a[...], w[one, 1])
-    own_a[...] = stream[0:half] + times(a[...], w[1, 1])
-    own_b[...] = stream[half : 2 * half] + times(b[...], w[1, 1])
-    for ref, tap in zip(side_b, taps_sent(plan, col)):
+    own[...] = stream[...] + times(a[...], w[1, 1])
+
+
+def far_b(plan, b, w, stream, own, *side):
+    col = lax.axis_index("col")
+    own[...] = stream[...] + times(b[...], w[1, 1])
+    for ref, tap in zip(side, taps_sent(plan, col)):
         ref[...] = times(b[...], w[1, tap])
 
 
@@ -429,14 +445,15 @@
     out_b[...] = own_b[...] + times(got_one[...], w[one, 1]) + times(got_two[...], w[two, 1])
 
 
-def far_four(n_side, own_a, own_b, from_above, from_below, *refs):
+def far_four(plan, n_side, own_a, own_b, back_one, back_two, *refs):
     side_b, (out_ref,) = refs[:n_side], refs[n_side:]
     half = own_a.shape[0]
-    out_ref[0:half] = own_a[...] + from_above[...].astype(jnp.float32) + from_below[...].astype(jnp.float32)
+    at_a, at_b = plan.starts(lax.axis_index("row"), half)
+    out_ref[pl.ds(at_a, half)] = own_a[...] + back_one[...].astype(jnp.float32) + back_two[...].astype(jnp.float32)
     total = own_b[...]
     for ref in side_b:
         total = total + ref[...].astype(jnp.float32)
-    out_ref[half : 2 * half] = total
+    out_ref[pl.ds(at_b, half)] = total
 
 
 def pair(value, hop, parity):
@@ -474,72 +491,89 @@
     ext, width, width4 = plan.ext, plan.width, plan.width4
     bf16, f32 = jnp.bfloat16, jnp.float32
     shape, vmem, dma = jax.ShapeDtypeStruct, pltpu.VMEM, pltpu.SemaphoreType.DMA
-    weights = inner_weights.reshape(inner_weights.shape[0], 9 * ch, ch)
-    if plan.two:
-        edge = lax.dynamic_slice_in_dim(features, (1 - col) * (tile_cols - ext), ext, axis=1)
-        sides = [cross(edge)]
-    else:
-        sides = [move(features[:, tile_cols - ext :], 0, 1), move(features[:, :ext], 0, -1)]
-    n_side = len(sides)
-    halo_shape = shape((halo, width, ch), bf16)
-    one, two = call(
-        functools.partial(gather_rows, plan, halo),
-        (halo_shape, halo_shape),
-        [dma((2 * (1 + n_side),))],
-        (features, *sides),
+    weights = pltpu.with_memory_space_constraint(inner_weights.reshape(inner_weights.shape[0], 9 * ch, ch), pltpu.HBM)
+    n_side = 1 if plan.two else 2
+    halo_shape, edge_shape = shape((halo, tile_cols, ch), bf16), shape((tile_rows, ext, ch), bf16)
+    tile, gains, *refs = call(
+        functools.partial(stage, plan, halo),
+        [shape(features.shape, bf16), shape(gains.shape, f32)] + [edge_shape] * n_side + [halo_shape] * 2,
+        [dma((4 + n_side,))],
+        tuple(pltpu.with_memory_space_constraint(value, pltpu.HBM) for value in (features, gains)),
         1,
-    )
+        any_args=(0, 1),
+    )
+    edges, (one, two) = refs[:n_side], refs[n_side:]
+
+    def spread_sides(values):
+        if plan.two:
+            return [cross(values[0])]
+        return [move(values[0], 0, 1), move(values[1], 0, -1)]
+
+    sides = spread_sides(edges)
     got_two, got_one = pair(two, 1, 1), pair(one, 1, 0)
     per_row = 2 * 9 * ch * ch
     whole = 9 * ch
     n_mid = tile_rows - 2 * d_two
     line = vmem((tile_rows, width + 2 * PAD, ch), f32)
     taps = vmem((tile_rows, width, 3 * ch), bf16)
-    mid, mid_act, edge_act, edge_base = call(
+    w_shape = shape((whole, ch), bf16)
+    base, taps1, w_one = call(
+        functools.partial(one_prepare, plan, halo),
+        (shape((tile_rows, width, ch), f32), shape((tile_rows, width, 3 * ch), bf16), w_shape),
+        [line, dma],
+        (tile, *sides, gains, weights),
+        per_row * 8 * width,
+        any_args=(2 + n_side,),
+    )
+    crossed = spread_sides(
+        call(
+            functools.partial(corners, plan),
+            [shape((2 * halo, ext, ch), bf16)] * n_side,
+            [dma((2 * n_side,))],
+            (got_one, got_two, taps1),
+            1,
+            any_args=(2,),
+        )
+    )
+    mid, mid_act, w_two = call(
         functools.partial(one_own, plan, halo),
-        (
-            shape((n_mid, width, ch), f32),
-            shape((n_mid, width, ch), bf16),
-            shape((2 * halo, width, ch), bf16),
-            shape((2 * halo, width, ch), f32),
-        ),
-        [vmem((tile_rows, width, ch), f32), line, taps, vmem((whole, ch), bf16), dma],
-        (features, *sides, weights, gains),
+        (shape((n_mid, width, ch), f32), shape((n_mid, width, ch), bf16), w_shape),
+        [dma],
+        (base, taps1, w_one, weights, gains),
         per_row * n_mid * width,
-        any_args=(1 + n_side,),
+        any_args=(3,),
     )
     sent = shape((d_three, width, ch), bf16)
-    stream2, act3, one, two = call(
+    stream2, taps3, one, two, w_three = call(
         functools.partial(one_two, plan, halo),
-        (shape((tile_rows, width, ch), f32), shape((tile_rows, width, ch), bf16), sent, sent),
+        (shape((tile_rows, width, ch), f32), shape((tile_rows, width, 3 * ch), bf16), sent, sent, w_shape),
         [
             vmem((4 * halo, width, ch), f32),
             vmem((n_mid + 2 * CHUNK, width + 2 * PAD, ch), f32),
             vmem((4 * halo, width, 3 * ch), bf16),
             vmem((2 * CHUNK, width, ch), f32),
             vmem((n_mid + 2 * CHUNK, width, 3 * ch), bf16),
-            vmem((whole, ch), bf16),
-            vmem((whole, ch), bf16),
-            dma((2,)),
+            dma,
         ],
-        (got_one, got_two, mid, mid_act, edge_act, edge_base, weights, gains),
+        (got_one, got_two, *crossed, mid, mid_act, taps1, base, w_one, w_two, weights, gains),
         per_row * (2 * CHUNK + tile_rows) * width,
-        any_args=(6,),
+        any_args=(8 + n_side,),
     )
     got_two, got_one = pair(two, 1, 1), pair(one, 1, 0)
     n_mid = tile_rows - 2 * d_three
     row_f32 = vmem((tile_rows, width, ch), f32)
-    edge, mid, mid_act = call(
+    edge, mid, mid_act, w_four = call(
         functools.partial(three_own, plan),
         (
             shape((2 * d_three, width, ch), f32),
             shape((n_mid, tile_cols, ch), f32),
             shape((n_mid, width4, ch), bf16),
+            w_shape,
         ),
-        [line, taps, row_f32, row_f32, vmem((whole, ch), bf16), dma],
-        (act3, weights, stream2, gains),
+        [row_f32, row_f32, dma],
+        (taps3, w_three, weights, stream2, gains),
         per_row * tile_rows * width,
-        any_args=(1,),
+        any_args=(2,),
     )
     sent = shape((d_four, width4, ch), bf16)
     stream3, act4, one, two = call(
@@ -548,14 +582,11 @@
         [
             vmem((2 * d_three, width + 2 * PAD, ch), f32),
             vmem((2 * d_three, width, 3 * ch), bf16),
-            vmem((2, 3 * ch, ch), bf16),
             vmem((2 * d_three, width, ch), f32),
             vmem((2 * d_three, width, ch), f32),
-            dma((2,)),
         ],
-        (got_one, got_two, edge, mid, mid_act, weights, gains),
+        (got_one, got_two, edge, mid, mid_act, w_three, gains),
         per_row * 2 * d_three * width / 3,
-        any_args=(5,),
     )
     got_two, got_one = pair(two, 1, 1), pair(one, 1, 0)
     line = vmem((tile_rows, width4 + 2 * PAD, ch), f32)
@@ -563,24 +594,27 @@
     acc4 = call(
         functools.partial(four_own, plan),
         shape((tile_rows, tile_cols, ch), f32),
-        [line, taps, vmem((whole, ch), bf16), dma],
-        (act4, weights, stream3),
+        [line, taps],
+        (act4, w_four, stream3),
         per_row * tile_rows * tile_cols,
-        any_args=(1,),
     )
     half = tile_rows // 2
-    stream4, a, b = call(
-        functools.partial(four_rim, plan),
-        (
-            shape((tile_rows, tile_cols, ch), f32),
-            shape((half, tile_cols, ch), bf16),
-            shape((half, tile_cols, ch), bf16),
-        ),
-        [line, taps, vmem((2, 3 * ch, ch), bf16), dma((2,))],
-        (got_one, got_two, acc4, weights, gains),
-        per_row * 2 * d_four * tile_cols / 3,
-        any_args=(3,),
-    )
+    if half != d_four or FAR // tile_rows % 2:
+        raise ValueError("tile rows")
+    finished = [
+        call(
+            functools.partial(four_rim, plan, k),
+            (shape((half, tile_cols, ch), f32), shape((half, tile_cols, ch), bf16)),
+            [
+                vmem((d_four, width4 + 2 * PAD, ch), f32),
+                vmem((d_four, tile_cols, 3 * ch), bf16),
+            ],
+            (got, acc4, w_four, gains),
+            per_row * d_four * tile_cols / 3,
+        )
+        for k, got in enumerate((got_one, got_two))
+    ]
+    (stream_a, a), (stream_b, b) = finished
     row_hop, col_hop = FAR // tile_rows, FAR // tile_cols
     if plan.two:
         crossed = [cross(a)]
@@ -590,12 +624,11 @@
     block = shape((half, tile_cols, ch), f32)
     sent = shape((half, tile_cols, ch), bf16)
     per_half = 2 * ch * ch * half * tile_cols
-    part_one, part_two, own_a, own_b, *side_b = call(
-        functools.partial(far_one, plan),
-        [block] * (4 + n_side),
-        [],
-        (a, b, far_weights, stream4),
-        per_half * 5,
+    part_one, part_two, own_a = call(
+        functools.partial(far_a, plan), [block] * 3, [], (a, far_weights, stream_a), per_half * 3
+    )
+    own_b, *side_b = call(
+        functools.partial(far_b, plan), [block] * (1 + n_side), [], (b, far_weights, stream_b), per_half * 2
     )
     one, two, *sides = call(
         functools.partial(far_two, plan, n_side),
@@ -617,7 +650,7 @@
         per_half * 3,
     )
     return call(
-        functools.partial(far_four, n_side),
+        functools.partial(far_four, plan, n_side),
         shape((tile_rows, tile_cols, ch), f32),
         [],
         (own_a, own_b, back_one, back_two, *side_got),

time: 91.9 us -> 81.4 us (0.89)
  Pallas kernels: 39.6 us -> 35.3 us
  starting transfers between devices: 22.8 us -> 19.4 us
  local copies, waits for them, and re-layouts: 2.79 us -> 0.01 us
    ppermute x3 -> x4, waiting for transfers between devices: 7.36 us -> 1.13 us  [cross(): return lax.ppermute(value, 'col', [(0, 1), (1, 0)])]
    ppermute x10, waiting for transfers between devices: 18.7 us -> 24.4 us  [pair(): return lax.ppermute(value, ('row', 'col'), ups + [(j, i) for i, j in ups])]
    pallas_call x11 -> x15, Pallas kernels: 39.6 us -> 35.3 us  [call(): pl.pallas_call(kernel, out_shape=out_shape, in_specs=[pl.BlockSpec(memory...]
    ppermute x10, starting transfers between devices: 19.9 us -> 16.8 us  [pair(): return lax.ppermute(value, ('row', 'col'), ups + [(j, i) for i, j in ups])]
    unnamed x8 -> x2, local copies, waits for them, and re-layouts: 1.84 us -> 0.01 us
    dynamic_slice x1 -> x0, local copies, waits for them, and re-layouts: 0.95 us -> none  [local(): lax.dynamic_slice_in_dim(features, (1 - col) * (tile_cols - ext), ext, ax...]
    ppermute x3 -> x4, starting transfers between devices: 2.86 us -> 2.61 us  [cross(): return lax.ppermute(value, 'col', [(0, 1), (1, 0)])]
  transfers between devices with their start and end apart: 13 -> 14, of which waited for: 9 -> 9; matrix products, arithmetic and copies ran while one was open for 0% -> 0% of each run, Pallas kernels for 21% -> 25%
where the time goes in v1:
time: 81.4 us; the launch traced here: 80.4 us
  Pallas kernels  35.3 us (43%)
  waiting for transfers between devices  25.5 us (31%)
  starting transfers between devices  19.4 us (24%)
    pallas_call x15, Pallas kernels, call(): pl.pallas_call(kernel, out_shape=out_shape, in_specs=[pl.BlockSpec(memory...  35.3 us
    ppermute x10, waiting for transfers between devices, pair(): return lax.ppermute(value, ('row', 'col'), ups + [(j, i) for i, j in ups])  24.4 us
    ppermute x10, starting transfers between devices, pair(): return lax.ppermute(value, ('row', 'col'), ups + [(j, i) for i, j in ups])  16.8 us
    ppermute x4, starting transfers between devices, cross(): return lax.ppermute(value, 'col', [(0, 1), (1, 0)])  2.61 us
  transfers between devices with their start and end apart: 14, of which 9 were waited for; matrix products, arithmetic and copies ran while one was open for 0% of the time, Pallas kernels for 25%

profile of v1, /device:TPU:9, one launch (start us, length us, event | category | flops | bytes accessed | tf_op | source)
XLA Modules:
  0.0 80.4 jit_solution(13646413253109366478)
XLA Ops:
  0.0 1.4 %shard_map.46 = (bf16[16,64,384]{2,1,0:T(8,128)(2,1)S(1)}, f32[5,384]{1,0:T(8,128)S(1)}, bf16[16,16,384]{2,1,0:T(8,128)(2,1)S(1)}, bf16[3,64,384]{2,1,0:T(8,128)(2,1)S(1)}, bf16[3,64,384]{2,1,0:T(8,128)(2,1)S(1)}) custom-call(bf16[16,64,384]{2,1,0:T(8,128)(2,1)} %features.1, f32[5,384]{1,0:T(8,128)} %gains.1), custom_call_target="tpu_custom_call" | custom-call | flops 1 | tf_op jit(solution)/shard_map/pallas_call | solution.py:377
  1.5 1.3 %collective-permute-start.2 = (bf16[16,16,384]{2,1,0:T(8,128)(2,1)S(1)}, bf16[16,16,384]{2,1,0:T(8,128)(2,1)S(1)}, u32[]{:S(2)}, u32[]{:S(2)}) collective-permute-start(bf16[16,16,384]{2,1,0:T(8,128)(2,1)S(1)} %get-tuple-element.46), channel_id=1, source_target_pairs={{0,1},{1,0},{2,3},{3,2},{4,5},{5,4},{6,7},{7,6},{8,9},{9,8},{10,11... | collective-permute-start | bytes 589832 | tf_op jit(solution)/shard_map/ppermute | solution.py:482
  2.7 1.0 %collective-permute-start = (bf16[3,64,384]{2,1,0:T(8,128)(2,1)S(1)}, bf16[3,64,384]{2,1,0:T(8,128)(2,1)S(1)}, u32[]{:S(2)}, u32[]{:S(2)}) collective-permute-start(bf16[3,64,384]{2,1,0:T(8,128)(2,1)S(1)} %get-tuple-element.43), channel_id=1, source_target_pairs={{0,2},{1,3},{4,6},{5,7},{8,10},{9,11},{12,14},{13,15},{16,18},{17,... | collective-permute-start | bytes 442376 | tf_op jit(solution)/shard_map/ppermute | solution.py:467
  3.7 3.0 %collective-permute-start.1 = (bf16[3,64,384]{2,1,0:T(8,128)(2,1)S(1)}, bf16[3,64,384]{2,1,0:T(8,128)(2,1)S(1)}, u32[]{:S(2)}, u32[]{:S(2)}) collective-permute-start(bf16[3,64,384]{2,1,0:T(8,128)(2,1)S(1)} %get-tuple-element.44), channel_id=1, source_target_pairs={{2,4},{3,5},{6,8},{7,9},{10,12},{11,13},{14,16},{15,17},{18,20},{1... | collective-permute-start | bytes 442376 | tf_op jit(solution)/shard_map/ppermute | solution.py:467
  6.7 0.6 collective-permute-done.2.refs_1_
  7.3 2.3 %shard_map.47 = (f32[16,80,384]{2,1,0:T(8,128)S(1)}, bf16[16,80,1152]{2,1,0:T(8,128)(2,1)S(1)}, bf16[3456,384]{1,0:T(8,128)(2,1)S(1)}) custom-call(bf16[16,64,384]{2,1,0:T(8,128)(2,1)S(1)} %get-tuple-element.45.refs_0_, bf16[16,16,384]{2,1,0:T(8,128)(2,1)S(1)} %collective-permute-done.2.refs_1_, f32[5,384]{1,0:T(8,128)S(1)} %get-tuple-element.47.refs_2_.gains.refs_10_, ...), custom_call_target="tpu_custom_call" | custom-call | flops 1698693120 | tf_op jit(solution)/shard_map/pallas_call | solution.py:377
  9.7 2.0 %collective-permute-done.1.two.refs_1_ = bf16[3,64,384]{2,1,0:T(8,128)(2,1)S(1)} collective-permute-done((bf16[3,64,384]{2,1,0:T(8,128)(2,1)S(1)}, bf16[3,64,384]{2,1,0:T(8,128)(2,1)S(1)}, u32[]{:S(2)}, u32[]{:S(2)}) %collective-permute-start.1) | collective-permute-done | bytes 147488 | tf_op jit(solution)/shard_map/ppermute | solution.py:467
  12.1 4.2 %shard_map.49 = (f32[12,80,384]{2,1,0:T(8,128)S(1)}, bf16[12,80,384]{2,1,0:T(8,128)(2,1)S(1)}, bf16[3456,384]{1,0:T(8,128)(2,1)S(1)}) custom-call(f32[16,80,384]{2,1,0:T(8,128)S(1)} %get-tuple-element.49.base.refs_6_, bf16[16,80,1152]{2,1,0:T(8,128)(2,1)S(1)} %get-tuple-element.48.after.taps.refs_5_, bf16[3456,384]{1,0:T(8,128)(2,1)S(1)} %get-tuple-element.50.w_one.refs_7_, ...), custom_call_target="tpu_custom_call" | custom-call | flops 2548039680 | tf_op jit(solution)/shard_map/pallas_call | solution.py:377
  16.3 9.3 %shard_map.50 = (f32[16,80,384]{2,1,0:T(8,128)S(1)}, bf16[16,80,1152]{2,1,0:T(8,128)(2,1)S(1)}, bf16[4,80,384]{2,1,0:T(8,128)(2,1)S(1)}, bf16[4,80,384]{2,1,0:T(8,128)(2,1)S(1)}, bf16[3456,384]{1,0:T(8,128)(2,1)S(1)}) custom-call(bf16[3,64,384]{2,1,0:T(8,128)(2,1)S(1)} %collective-permute-done.one.refs_0_, ...), custom_call_target="tpu_custom_call" | custom-call | flops 5096079360 | tf_op jit(solution)/shard_map/pallas_call | solution.py:377
  25.6 0.8 %collective-permute-start.4 = (bf16[4,80,384]{2,1,0:T(8,128)(2,1)S(1)}, bf16[4,80,384]{2,1,0:T(8,128)(2,1)S(1)}, u32[]{:S(2)}, u32[]{:S(2)}) collective-permute-start(bf16[4,80,384]{2,1,0:T(8,128)(2,1)S(1)} %get-tuple-element.54), channel_id=1, source_target_pairs={{0,2},{1,3},{4,6},{5,7},{8,10},{9,11},{12,14},{13,15},{16,18},{17,... | collective-permute-start | bytes 737288 | tf_op jit(solution)/shard_map/ppermute | solution.py:467
  26.4 3.2 %collective-permute-start.5 = (bf16[4,80,384]{2,1,0:T(8,128)(2,1)S(1)}, bf16[4,80,384]{2,1,0:T(8,128)(2,1)S(1)}, u32[]{:S(2)}, u32[]{:S(2)}) collective-permute-start(bf16[4,80,384]{2,1,0:T(8,128)(2,1)S(1)} %get-tuple-element.55), channel_id=1, source_target_pairs={{2,4},{3,5},{6,8},{7,9},{10,12},{11,13},{14,16},{15,17},{18,20},{1... | collective-permute-start | bytes 737288 | tf_op jit(solution)/shard_map/ppermute | solution.py:467
  29.7 5.2 %shard_map.51 = (f32[8,80,384]{2,1,0:T(8,128)S(1)}, f32[8,64,384]{2,1,0:T(8,128)S(1)}, bf16[8,72,384]{2,1,0:T(8,128)(2,1)S(1)}, bf16[3456,384]{1,0:T(8,128)(2,1)S(1)}) custom-call(bf16[16,80,1152]{2,1,0:T(8,128)(2,1)S(1)} %get-tuple-element.56.taps, bf16[3456,384]{1,0:T(8,128)(2,1)S(1)} %get-tuple-element.57.weight, bf16[4,3456,384]{2,1,0:T(8,128)(2,1)} %bitcast.4, ...), custom_call_target="tpu_custom_call" | custom-call | flops 3397386240 | tf_op jit(solution)/shard_map/pallas_call | solution.py:377
  34.8 1.7 %collective-permute-done.5.got_two = bf16[4,80,384]{2,1,0:T(8,128)(2,1)S(1)} collective-permute-done((bf16[4,80,384]{2,1,0:T(8,128)(2,1)S(1)}, bf16[4,80,384]{2,1,0:T(8,128)(2,1)S(1)}, u32[]{:S(2)}, u32[]{:S(2)}) %collective-permute-start.5) | collective-permute-done | bytes 245792 | tf_op jit(solution)/shard_map/ppermute | solution.py:467
  36.6 2.1 %shard_map.52 = (f32[16,64,384]{2,1,0:T(8,128)S(1)}, bf16[16,72,384]{2,1,0:T(8,128)(2,1)S(1)}, bf16[8,72,384]{2,1,0:T(8,128)(2,1)S(1)}, bf16[8,72,384]{2,1,0:T(8,128)(2,1)S(1)}) custom-call(bf16[4,80,384]{2,1,0:T(8,128)(2,1)S(1)} %collective-permute-done.4.got_one, bf16[4,80,384]{2,1,0:T(8,128)(2,1)S(1)} %collective-permute-done.5.got_two, ...), custom_call_target="tpu_custom_call" | custom-call | flops 566231040 | tf_op jit(solution)/shard_map/pallas_call | solution.py:377
  38.7 3.1 %collective-permute-start.8 = (bf16[8,72,384]{2,1,0:T(8,128)(2,1)S(1)}, bf16[8,72,384]{2,1,0:T(8,128)(2,1)S(1)}, u32[]{:S(2)}, u32[]{:S(2)}) collective-permute-start(bf16[8,72,384]{2,1,0:T(8,128)(2,1)S(1)} %get-tuple-element.67), channel_id=1, source_target_pairs={{2,4},{3,5},{6,8},{7,9},{10,12},{11,13},{14,16},{15,17},{18,20},{1... | collective-permute-start | bytes 1327112 | tf_op jit(solution)/shard_map/ppermute | solution.py:467
  41.8 3.1 %shard_map.53.acc = f32[16,64,384]{2,1,0:T(8,128)S(1)} custom-call(bf16[16,72,384]{2,1,0:T(8,128)(2,1)S(1)} %get-tuple-element.63.act, bf16[3456,384]{1,0:T(8,128)(2,1)S(1)} %get-tuple-element.64.weight, f32[16,64,384]{2,1,0:T(8,128)S(1)} %get-tuple-element.65.stream), custom_call_target="tpu_custom_call" | custom-call | flops 2717908992 | tf_op jit(solution)/shard_map/pallas_call | solution.py:377
  44.9 1.4 %shard_map.54 = (f32[8,64,384]{2,1,0:T(8,128)S(1)}, bf16[8,64,384]{2,1,0:T(8,128)(2,1)S(1)}) custom-call(bf16[8,72,384]{2,1,0:T(8,128)(2,1)S(1)} %collective-permute-done.6.got, f32[16,64,384]{2,1,0:T(8,128)S(1)} %shard_map.53.acc, bf16[3456,384]{1,0:T(8,128)(2,1)S(1)} %get-tuple-element.64.weight, f32[5,384]{1,0:T(8,128)S(1)} %get-tuple-element.47.refs_2_.gains.refs_10_), custom_call_target="tpu_custom_call" | custom-call | flops 452984832 | tf_op jit(solution)/shard_map/pallas_call | solution.py:377
  46.7 6.7 %collective-permute-done.8.got = bf16[8,72,384]{2,1,0:T(8,128)(2,1)S(1)} collective-permute-done((bf16[8,72,384]{2,1,0:T(8,128)(2,1)S(1)}, bf16[8,72,384]{2,1,0:T(8,128)(2,1)S(1)}, u32[]{:S(2)}, u32[]{:S(2)}) %collective-permute-start.8) | collective-permute-done | bytes 442400 | tf_op jit(solution)/shard_map/ppermute | solution.py:467
  53.4 1.4 %shard_map.55 = (f32[8,64,384]{2,1,0:T(8,128)S(1)}, bf16[8,64,384]{2,1,0:T(8,128)(2,1)S(1)}) custom-call(bf16[8,72,384]{2,1,0:T(8,128)(2,1)S(1)} %collective-permute-done.8.got, f32[16,64,384]{2,1,0:T(8,128)S(1)} %shard_map.53.acc, bf16[3456,384]{1,0:T(8,128)(2,1)S(1)} %get-tuple-element.64.weight, f32[5,384]{1,0:T(8,128)S(1)} %get-tuple-element.47.refs_2_.gains.refs_10_), custom_call_target="tpu_custom_call" | custom-call | flops 452984832 | tf_op jit(solution)/shard_map/pallas_call | solution.py:377
  54.8 3.4 %collective-permute-start.10 = (bf16[8,64,384]{2,1,0:T(8,128)(2,1)S(1)}, bf16[8,64,384]{2,1,0:T(8,128)(2,1)S(1)}, u32[]{:S(2)}, u32[]{:S(2)}) collective-permute-start(bf16[8,64,384]{2,1,0:T(8,128)(2,1)S(1)} %get-tuple-element.68.b), channel_id=1, source_target_pairs={{8,16},{9,17},{10,18},{11,19},{12,20},{13,21},{14,22},{15,23},{16,... | collective-permute-start | bytes 1179656 | tf_op jit(solution)/shard_map/ppermute | solution.py:467
  58.3 0.7 shard_map.57
  58.9 0.9 %shard_map.56 = (f32[8,64,384]{2,1,0:T(8,128)S(1)}, f32[8,64,384]{2,1,0:T(8,128)S(1)}, f32[8,64,384]{2,1,0:T(8,128)S(1)}) custom-call(bf16[8,64,384]{2,1,0:T(8,128)(2,1)S(1)} %get-tuple-element.66.a, bf16[3,3,384,384]{3,2,1,0:T(8,128)(2,1)S(1)} %copy-done, f32[8,64,384]{2,1,0:T(8,128)S(1)} %get-tuple-element.69.stream), custom_call_target="tpu_custom_call" | custom-call | flops 452984832 | tf_op jit(solution)/shard_map/pallas_call | solution.py:377
  59.9 4.5 %collective-permute-done.10.refs_2_ = bf16[8,64,384]{2,1,0:T(8,128)(2,1)S(1)} collective-permute-done((bf16[8,64,384]{2,1,0:T(8,128)(2,1)S(1)}, bf16[8,64,384]{2,1,0:T(8,128)(2,1)S(1)}, u32[]{:S(2)}, u32[]{:S(2)}) %collective-permute-start.10) | collective-permute-done | bytes 393248 | tf_op jit(solution)/shard_map/ppermute | solution.py:467
  64.4 1.9 %collective-permute-done.9.refs_1_ = bf16[8,64,384]{2,1,0:T(8,128)(2,1)S(1)} collective-permute-done((bf16[8,64,384]{2,1,0:T(8,128)(2,1)S(1)}, bf16[8,64,384]{2,1,0:T(8,128)(2,1)S(1)}, u32[]{:S(2)}, u32[]{:S(2)}) %collective-permute-start.9) | collective-permute-done | bytes 393248 | tf_op jit(solution)/shard_map/ppermute | solution.py:467
  66.3 1.1 %shard_map.59 = (bf16[8,64,384]{2,1,0:T(8,128)(2,1)S(1)}, bf16[8,64,384]{2,1,0:T(8,128)(2,1)S(1)}, bf16[8,64,384]{2,1,0:T(8,128)(2,1)S(1)}) custom-call(bf16[8,64,384]{2,1,0:T(8,128)(2,1)S(1)} %collective-permute-done.7.refs_0_, bf16[8,64,384]{2,1,0:T(8,128)(2,1)S(1)} %collective-permute-done.9.refs_1_, ...), custom_call_target="tpu_custom_call" | custom-call | flops 603979776 | tf_op jit(solution)/shard_map/pallas_call | solution.py:377
  67.5 2.1 %collective-permute-start.12 = (bf16[8,64,384]{2,1,0:T(8,128)(2,1)S(1)}, bf16[8,64,384]{2,1,0:T(8,128)(2,1)S(1)}, u32[]{:S(2)}, u32[]{:S(2)}) collective-permute-start(bf16[8,64,384]{2,1,0:T(8,128)(2,1)S(1)} %get-tuple-element.79), channel_id=1, source_target_pairs={{8,16},{9,17},{10,18},{11,19},{12,20},{13,21},{14,22},{15,23},{16,... | collective-permute-start | bytes 1179656 | tf_op jit(solution)/shard_map/ppermute | solution.py:467
  69.6 0.6 collective-permute-start.13
  70.2 0.9 %shard_map.58 = (f32[8,64,384]{2,1,0:T(8,128)S(1)}, f32[8,64,384]{2,1,0:T(8,128)S(1)}) custom-call(bf16[8,64,384]{2,1,0:T(8,128)(2,1)S(1)} %collective-permute-done.7.refs_0_, bf16[8,64,384]{2,1,0:T(8,128)(2,1)S(1)} %collective-permute-done.9.refs_1_, bf16[8,64,384]{2,1,0:T(8,128)(2,1)S(1)} %collective-permute-done.10.refs_2_, ...), custom_call_target="tpu_custom_call" | custom-call | flops 452984832 | tf_op jit(solution)/shard_map/pallas_call | solution.py:377
  71.1 5.8 %collective-permute-done.11.back_one = bf16[8,64,384]{2,1,0:T(8,128)(2,1)S(1)} collective-permute-done((bf16[8,64,384]{2,1,0:T(8,128)(2,1)S(1)}, bf16[8,64,384]{2,1,0:T(8,128)(2,1)S(1)}, u32[]{:S(2)}, u32[]{:S(2)}) %collective-permute-start.11) | collective-permute-done | bytes 393248 | tf_op jit(solution)/shard_map/ppermute | solution.py:467
  77.0 1.6 %collective-permute-done.12.back_two = bf16[8,64,384]{2,1,0:T(8,128)(2,1)S(1)} collective-permute-done((bf16[8,64,384]{2,1,0:T(8,128)(2,1)S(1)}, bf16[8,64,384]{2,1,0:T(8,128)(2,1)S(1)}, u32[]{:S(2)}, u32[]{:S(2)}) %collective-permute-start.12) | collective-permute-done | bytes 393248 | tf_op jit(solution)/shard_map/ppermute | solution.py:467
  78.6 0.5 collective-permute-done.13.refs_0_
  79.1 1.3 %shard_map.60 = f32[16,64,384]{2,1,0:T(8,128)} custom-call(f32[8,64,384]{2,1,0:T(8,128)S(1)} %get-tuple-element.73.own_a, f32[8,64,384]{2,1,0:T(8,128)S(1)} %get-tuple-element.74.own_b, bf16[8,64,384]{2,1,0:T(8,128)(2,1)S(1)} %collective-permute-done.11.back_one, bf16[8,64,384]{2,1,0:T(8,128)(2,1)S(1)} %collective-permute-done.12.back_two, ...), custom_call_target="tpu_custom_call" | custom-call | flops 1 | tf_op jit(solution)/shard_map/pallas_call | solution.py:377
  (13 shorter events, 1.0 us)
Async XLA Ops:
  1.5 5.9 %collective-permute-start.2 = (bf16[16,16,384]{2,1,0:T(8,128)(2,1)S(1)}, bf16[16,16,384]{2,1,0:T(8,128)(2,1)S(1)}, u32[]{:S(2)}, u32[]{:S(2)}) collective-permute-start(bf16[16,16,384]{2,1,0:T(8,128)(2,1)S(1)} %get-tuple-element.46), channel_id=1, source_target_pairs={{0,1},{1,0},{2,3},{3,2},{4,5},{5,4},{6,7},{7,6},{8,9},{9,8},{10,11... | collective-permute-start | bytes 589832 | tf_op jit(solution)/shard_map/ppermute | solution.py:482
  2.7 6.9 %collective-permute-start = (bf16[3,64,384]{2,1,0:T(8,128)(2,1)S(1)}, bf16[3,64,384]{2,1,0:T(8,128)(2,1)S(1)}, u32[]{:S(2)}, u32[]{:S(2)}) collective-permute-start(bf16[3,64,384]{2,1,0:T(8,128)(2,1)S(1)} %get-tuple-element.43), channel_id=1, source_target_pairs={{0,2},{1,3},{4,6},{5,7},{8,10},{9,11},{12,14},{13,15},{16,18},{17,... | collective-permute-start | bytes 442376 | tf_op jit(solution)/shard_map/ppermute | solution.py:467
  3.7 8.0 %collective-permute-start.1 = (bf16[3,64,384]{2,1,0:T(8,128)(2,1)S(1)}, bf16[3,64,384]{2,1,0:T(8,128)(2,1)S(1)}, u32[]{:S(2)}, u32[]{:S(2)}) collective-permute-start(bf16[3,64,384]{2,1,0:T(8,128)(2,1)S(1)} %get-tuple-element.44), channel_id=1, source_target_pairs={{2,4},{3,5},{6,8},{7,9},{10,12},{11,13},{14,16},{15,17},{18,20},{1... | collective-permute-start | bytes 442376 | tf_op jit(solution)/shard_map/ppermute | solution.py:467
  11.8 4.5 %collective-permute-start.3 = (bf16[6,16,384]{2,1,0:T(8,128)(2,1)S(1)}, bf16[6,16,384]{2,1,0:T(8,128)(2,1)S(1)}, u32[]{:S(2)}, u32[]{:S(2)}) collective-permute-start(bf16[6,16,384]{2,1,0:T(8,128)(2,1)S(1)} %shard_map.48), channel_id=1, source_target_pairs={{0,1},{1,0},{2,3},{3,2},{4,5},{5,4},{6,7},{7,6},{8,9},{9,8},{10,11... | collective-permute-start | bytes 221192 | tf_op jit(solution)/shard_map/ppermute | solution.py:482
  25.6 9.2 %collective-permute-start.4 = (bf16[4,80,384]{2,1,0:T(8,128)(2,1)S(1)}, bf16[4,80,384]{2,1,0:T(8,128)(2,1)S(1)}, u32[]{:S(2)}, u32[]{:S(2)}) collective-permute-start(bf16[4,80,384]{2,1,0:T(8,128)(2,1)S(1)} %get-tuple-element.54), channel_id=1, source_target_pairs={{0,2},{1,3},{4,6},{5,7},{8,10},{9,11},{12,14},{13,15},{16,18},{17,... | collective-permute-start | bytes 737288 | tf_op jit(solution)/shard_map/ppermute | solution.py:467
  26.4 10.1 %collective-permute-start.5 = (bf16[4,80,384]{2,1,0:T(8,128)(2,1)S(1)}, bf16[4,80,384]{2,1,0:T(8,128)(2,1)S(1)}, u32[]{:S(2)}, u32[]{:S(2)}) collective-permute-start(bf16[4,80,384]{2,1,0:T(8,128)(2,1)S(1)} %get-tuple-element.55), channel_id=1, source_target_pairs={{2,4},{3,5},{6,8},{7,9},{10,12},{11,13},{14,16},{15,17},{18,20},{1... | collective-permute-start | bytes 737288 | tf_op jit(solution)/shard_map/ppermute | solution.py:467
  38.6 6.3 %collective-permute-start.6 = (bf16[8,72,384]{2,1,0:T(8,128)(2,1)S(1)}, bf16[8,72,384]{2,1,0:T(8,128)(2,1)S(1)}, u32[]{:S(2)}, u32[]{:S(2)}) collective-permute-start(bf16[8,72,384]{2,1,0:T(8,128)(2,1)S(1)} %get-tuple-element.62), channel_id=1, source_target_pairs={{0,2},{1,3},{4,6},{5,7},{8,10},{9,11},{12,14},{13,15},{16,18},{17,... | collective-permute-start | bytes 1327112 | tf_op jit(solution)/shard_map/ppermute | solution.py:467
  38.7 14.7 %collective-permute-start.8 = (bf16[8,72,384]{2,1,0:T(8,128)(2,1)S(1)}, bf16[8,72,384]{2,1,0:T(8,128)(2,1)S(1)}, u32[]{:S(2)}, u32[]{:S(2)}) collective-permute-start(bf16[8,72,384]{2,1,0:T(8,128)(2,1)S(1)} %get-tuple-element.67), channel_id=1, source_target_pairs={{2,4},{3,5},{6,8},{7,9},{10,12},{11,13},{14,16},{15,17},{18,20},{1... | collective-permute-start | bytes 1327112 | tf_op jit(solution)/shard_map/ppermute | solution.py:467
  46.3 12.0 %copy-start = (bf16[3,3,384,384]{3,2,1,0:T(8,128)(2,1)S(1)}, bf16[3,3,384,384]{3,2,1,0:T(8,128)(2,1)}, u32[]{:S(2)}) copy-start(bf16[3,3,384,384]{3,2,1,0:T(8,128)(2,1)} %refs_3_.3) | copy-start | bytes 7962628
  46.3 13.5 %collective-permute-start.7 = (bf16[8,64,384]{2,1,0:T(8,128)(2,1)S(1)}, bf16[8,64,384]{2,1,0:T(8,128)(2,1)S(1)}, u32[]{:S(2)}, u32[]{:S(2)}) collective-permute-start(bf16[8,64,384]{2,1,0:T(8,128)(2,1)S(1)} %get-tuple-element.66.a), channel_id=1, source_target_pairs={{0,1},{1,0},{2,3},{3,2},{4,5},{5,4},{6,7},{7,6},{8,9},{9,8},{10,11... | collective-permute-start | bytes 1179656 | tf_op jit(solution)/shard_map/ppermute | solution.py:482
  54.8 9.6 %collective-permute-start.10 = (bf16[8,64,384]{2,1,0:T(8,128)(2,1)S(1)}, bf16[8,64,384]{2,1,0:T(8,128)(2,1)S(1)}, u32[]{:S(2)}, u32[]{:S(2)}) collective-permute-start(bf16[8,64,384]{2,1,0:T(8,128)(2,1)S(1)} %get-tuple-element.68.b), channel_id=1, source_target_pairs={{8,16},{9,17},{10,18},{11,19},{12,20},{13,21},{14,22},{15,23},{16,... | collective-permute-start | bytes 1179656 | tf_op jit(solution)/shard_map/ppermute | solution.py:467
  58.2 8.1 %collective-permute-start.9 = (bf16[8,64,384]{2,1,0:T(8,128)(2,1)S(1)}, bf16[8,64,384]{2,1,0:T(8,128)(2,1)S(1)}, u32[]{:S(2)}, u32[]{:S(2)}) collective-permute-start(bf16[8,64,384]{2,1,0:T(8,128)(2,1)S(1)} %get-tuple-element.68.b), channel_id=1, source_target_pairs={{0,8},{1,9},{2,10},{3,11},{4,12},{5,13},{6,14},{7,15},{16,24},{17,... | collective-permute-start | bytes 1179656 | tf_op jit(solution)/shard_map/ppermute | solution.py:467
  67.4 9.5 %collective-permute-start.11 = (bf16[8,64,384]{2,1,0:T(8,128)(2,1)S(1)}, bf16[8,64,384]{2,1,0:T(8,128)(2,1)S(1)}, u32[]{:S(2)}, u32[]{:S(2)}) collective-permute-start(bf16[8,64,384]{2,1,0:T(8,128)(2,1)S(1)} %get-tuple-element.78), channel_id=1, source_target_pairs={{0,8},{1,9},{2,10},{3,11},{4,12},{5,13},{6,14},{7,15},{16,24},{17,... | collective-permute-start | bytes 1179656 | tf_op jit(solution)/shard_map/ppermute | solution.py:467
  67.5 11.1 %collective-permute-start.12 = (bf16[8,64,384]{2,1,0:T(8,128)(2,1)S(1)}, bf16[8,64,384]{2,1,0:T(8,128)(2,1)S(1)}, u32[]{:S(2)}, u32[]{:S(2)}) collective-permute-start(bf16[8,64,384]{2,1,0:T(8,128)(2,1)S(1)} %get-tuple-element.79), channel_id=1, source_target_pairs={{8,16},{9,17},{10,18},{11,19},{12,20},{13,21},{14,22},{15,23},{16,... | collective-permute-start | bytes 1179656 | tf_op jit(solution)/shard_map/ppermute | solution.py:467
  69.6 9.5 %collective-permute-start.13 = (bf16[8,64,384]{2,1,0:T(8,128)(2,1)S(1)}, bf16[8,64,384]{2,1,0:T(8,128)(2,1)S(1)}, u32[]{:S(2)}, u32[]{:S(2)}) collective-permute-start(bf16[8,64,384]{2,1,0:T(8,128)(2,1)S(1)} %get-tuple-element.80), channel_id=1, source_target_pairs={{0,1},{1,0},{2,3},{3,2},{4,5},{5,4},{6,7},{7,6},{8,9},{9,8},{10,11... | collective-permute-start | bytes 1179656 | tf_op jit(solution)/shard_map/ppermute | solution.py:482

commit v2 on v1

--- a/solution.py
+++ b/solution.py
@@ -6,6 +6,7 @@
 from jax.experimental import pallas as pl
 from jax.experimental.pallas import tpu as pltpu
 from jax.sharding import PartitionSpec as P
+
 
 FAR = 64
 DILATIONS = (1, 2, 4, 8)
@@ -114,14 +115,12 @@
         body(row)
 
 
-def stage(plan, halo, features, gains, *refs):
+def stage(plan, halo, features, *refs):
     n_side = 1 if plan.two else 2
-    tile, gains_out = refs[:2]
-    edges, outs, (sems,) = refs[2 : 2 + n_side], refs[2 + n_side : 4 + n_side], refs[4 + n_side :]
+    edges, outs, (sems,) = refs[:n_side], refs[n_side : 2 + n_side], refs[2 + n_side :]
     row_id, col = lax.axis_index("row"), lax.axis_index("col")
     moves = [(features.at[:, pl.ds(at, plan.ext)], edge) for at, edge in zip(plan.edges(col), edges)]
     moves += [(features.at[pl.ds(at, halo)], out) for at, out in zip(plan.starts(row_id, halo), outs)]
-    moves += [(gains, gains_out), (features, tile)]
     copies = [pltpu.make_async_copy(src, dst, sems.at[k]) for k, (src, dst) in enumerate(moves)]
     for copy in copies:
         copy.start()
@@ -151,29 +150,34 @@
 CHUNK = 4
 
 
-def one_prepare(plan, halo, *refs):
+def one_prepare(plan, *refs):
     n_side = 1 if plan.two else 2
-    parts = refs[: 1 + n_side]
-    gains, w_hbm, base, taps, w_one, line, sem = refs[1 + n_side :]
-    copy = fetch(w_hbm, 0, w_one, sem)
-    copy.start()
-    col = lax.axis_index("col")
+    features, sides = refs[0], refs[1 : 1 + n_side]
+    gains_hbm, w_hbm, base, taps, w_one, gains, tile, line, sems = refs[1 + n_side :]
+    moves = ((features, tile), (gains_hbm, gains), (w_hbm.at[0], w_one))
+    copies = [pltpu.make_async_copy(src, dst, sems.at[k]) for k, (src, dst) in enumerate(moves)]
+    for copy in copies:
+        copy.start()
+    col = lax.axis_index("col")
+    parts = (tile,) + tuple(sides)
+    clear_edges(line)
+    for copy in copies[:2]:
+        copy.wait()
     for part, offset in zip(parts, (plan.own(col),) + plan.sides(col)):
         base[:, pl.ds(offset, part.shape[1]), :] = part[...].astype(jnp.float32)
-    clear_edges(line)
 
     def prepare(row):
         lay(line, taps, row, plan.inside(col, normed(base[row], gains[0:1, :])), DILATIONS[0], PAD, plan.width)
 
     rows_of(plan.tile_rows, prepare)
-    copy.wait()
+    copies[2].wait()
 
 
 def fetch(w_hbm, layer, out, sem):
     return pltpu.make_async_copy(w_hbm.at[layer], out, sem)
 
 
-def one_own(plan, halo, base, taps, w_one, w_hbm, gains, mid, mid_act, w_next, sem):
+def one_own(plan, base, taps, w_one, w_hbm, gains, mid, mid_act, w_next, sem):
     col = lax.axis_index("col")
     copy = fetch(w_hbm, 1, w_next, sem)
     copy.start()
@@ -373,7 +377,7 @@
     return jnp.dot(a.reshape(rows * cols, ch), w, preferred_element_type=jnp.float32).reshape(rows, cols, ch)
 
 
-def call(kernel, out_shape, scratch, args, flops, any_args=()):
+def call(kernel, out_shape, scratch, args, flops, any_args=(), out_space=pltpu.VMEM):
     return pl.pallas_call(
         kernel,
         out_shape=out_shape,
@@ -381,7 +385,7 @@
             pl.BlockSpec(memory_space=pltpu.HBM) if k in any_args else pl.BlockSpec(memory_space=pltpu.VMEM)
             for k in range(len(args))
         ],
-        out_specs=jax.tree.map(lambda _: pl.BlockSpec(memory_space=pltpu.VMEM), out_shape),
+        out_specs=jax.tree.map(lambda _: pl.BlockSpec(memory_space=out_space), out_shape),
         scratch_shapes=scratch,
         compiler_params=pltpu.CompilerParams(vmem_limit_bytes=VMEM_LIMIT),
         cost_estimate=pl.CostEstimate(flops=int(flops), transcendentals=0, bytes_accessed=0),
@@ -446,14 +450,21 @@
 
 
 def far_four(plan, n_side, own_a, own_b, back_one, back_two, *refs):
-    side_b, (out_ref,) = refs[:n_side], refs[n_side:]
+    side_b, (out_ref, held, sems) = refs[:n_side], refs[n_side:]
     half = own_a.shape[0]
     at_a, at_b = plan.starts(lax.axis_index("row"), half)
-    out_ref[pl.ds(at_a, half)] = own_a[...] + back_one[...].astype(jnp.float32) + back_two[...].astype(jnp.float32)
+    copies = [
+        pltpu.make_async_copy(held.at[k], out_ref.at[pl.ds(at, half)], sems.at[k]) for k, at in enumerate((at_a, at_b))
+    ]
+    held[0] = own_a[...] + back_one[...].astype(jnp.float32) + back_two[...].astype(jnp.float32)
+    copies[0].start()
     total = own_b[...]
     for ref in side_b:
         total = total + ref[...].astype(jnp.float32)
-    out_ref[pl.ds(at_b, half)] = total
+    held[1] = total
+    copies[1].start()
+    for copy in copies:
+        copy.wait()
 
 
 def pair(value, hop, parity):
@@ -467,6 +478,12 @@
     return lax.ppermute(value, ("row", "col"), ups + [(j, i) for i, j in ups])
 
 
+def row_swap(one, two):
+    got_two = pair(two, 1, 1)
+    got_one = pair(one, 1, 0)
+    return got_one, got_two
+
+
 def move(value, rows, cols):
     n_row, n_col = lax.axis_size("row"), lax.axis_size("col")
     pairs = [
@@ -485,22 +502,22 @@
 def local(features, inner_weights, far_weights, gains):
     tile_rows, tile_cols, ch = features.shape
     plan = Plan(tile_rows, tile_cols, ch, lax.axis_size("row"), lax.axis_size("col"))
-    col = lax.axis_index("col")
     d_one, d_two, d_three, d_four = DILATIONS
     halo = d_one + d_two
     ext, width, width4 = plan.ext, plan.width, plan.width4
     bf16, f32 = jnp.bfloat16, jnp.float32
     shape, vmem, dma = jax.ShapeDtypeStruct, pltpu.VMEM, pltpu.SemaphoreType.DMA
+    features, gains = [pltpu.with_memory_space_constraint(value, pltpu.HBM) for value in (features, gains)]
     weights = pltpu.with_memory_space_constraint(inner_weights.reshape(inner_weights.shape[0], 9 * ch, ch), pltpu.HBM)
     n_side = 1 if plan.two else 2
     halo_shape, edge_shape = shape((halo, tile_cols, ch), bf16), shape((tile_rows, ext, ch), bf16)
-    tile, gains, *refs = call(
+    refs = call(
         functools.partial(stage, plan, halo),
-        [shape(features.shape, bf16), shape(gains.shape, f32)] + [edge_shape] * n_side + [halo_shape] * 2,
-        [dma((4 + n_side,))],
-        tuple(pltpu.with_memory_space_constraint(value, pltpu.HBM) for value in (features, gains)),
+        [edge_shape] * n_side + [halo_shape] * 2,
+        [dma((2 + n_side,))],
+        (features,),
         1,
-        any_args=(0, 1),
+        any_args=(0,),
     )
     edges, (one, two) = refs[:n_side], refs[n_side:]
 
@@ -510,20 +527,20 @@
         return [move(values[0], 0, 1), move(values[1], 0, -1)]
 
     sides = spread_sides(edges)
-    got_two, got_one = pair(two, 1, 1), pair(one, 1, 0)
+    got_one, got_two = row_swap(one, two)
     per_row = 2 * 9 * ch * ch
     whole = 9 * ch
     n_mid = tile_rows - 2 * d_two
     line = vmem((tile_rows, width + 2 * PAD, ch), f32)
     taps = vmem((tile_rows, width, 3 * ch), bf16)
     w_shape = shape((whole, ch), bf16)
-    base, taps1, w_one = call(
-        functools.partial(one_prepare, plan, halo),
-        (shape((tile_rows, width, ch), f32), shape((tile_rows, width, 3 * ch), bf16), w_shape),
-        [line, dma],
-        (tile, *sides, gains, weights),
+    base, taps1, w_one, gains = call(
+        functools.partial(one_prepare, plan),
+        (shape((tile_rows, width, ch), f32), shape((tile_rows, width, 3 * ch), bf16), w_shape, shape(gains.shape, f32)),
+        [vmem(features.shape, bf16), line, dma((3,))],
+        (features, *sides, gains, weights),
         per_row * 8 * width,
-        any_args=(2 + n_side,),
+        any_args=(0, 1 + n_side, 2 + n_side),
     )
     crossed = spread_sides(
         call(
@@ -536,7 +553,7 @@
         )
     )
     mid, mid_act, w_two = call(
-        functools.partial(one_own, plan, halo),
+        functools.partial(one_own, plan),
         (shape((n_mid, width, ch), f32), shape((n_mid, width, ch), bf16), w_shape),
         [dma],
         (base, taps1, w_one, weights, gains),
@@ -559,7 +576,7 @@
         per_row * (2 * CHUNK + tile_rows) * width,
         any_args=(8 + n_side,),
     )
-    got_two, got_one = pair(two, 1, 1), pair(one, 1, 0)
+    got_one, got_two = row_swap(one, two)
     n_mid = tile_rows - 2 * d_three
     row_f32 = vmem((tile_rows, width, ch), f32)
     edge, mid, mid_act, w_four = call(
@@ -588,7 +605,7 @@
         (got_one, got_two, edge, mid, mid_act, w_three, gains),
         per_row * 2 * d_three * width / 3,
     )
-    got_two, got_one = pair(two, 1, 1), pair(one, 1, 0)
+    got_one, got_two = row_swap(one, two)
     line = vmem((tile_rows, width4 + 2 * PAD, ch), f32)
     taps = vmem((tile_rows, tile_cols, 3 * ch), bf16)
     acc4 = call(
@@ -652,9 +669,10 @@
     return call(
         functools.partial(far_four, plan, n_side),
         shape((tile_rows, tile_cols, ch), f32),
-        [],
+        [vmem((2, half, tile_cols, ch), f32), dma((2,))],
         (own_a, own_b, back_one, back_two, *side_got),
         1,
+        out_space=pltpu.HBM,
     )
 
 

time: 81.4 us -> 82.3 us (1.011)
  starting transfers between devices: 19.4 us -> 20.3 us
  waiting for transfers between devices: 25.5 us -> 24.6 us
    ppermute x10, starting transfers between devices: 16.8 us -> 17.8 us  [pair(): return lax.ppermute(value, ('row', 'col'), ups + [(j, i) for i, j in ups])]
    ppermute x10, waiting for transfers between devices: 24.4 us -> 23.5 us  [pair(): return lax.ppermute(value, ('row', 'col'), ups + [(j, i) for i, j in ups])]
  transfers between devices with their start and end apart: 14 -> 14, of which waited for: 9 -> 9; matrix products, arithmetic and copies ran while one was open for 0% -> 0% of each run, Pallas kernels for 25% -> 26%
where the time goes in v2:
time: 82.3 us; the launch traced here: 81.4 us
  Pallas kernels  36 us (44%)
  waiting for transfers between devices  24.6 us (30%)
  starting transfers between devices  20.3 us (25%)
    pallas_call x15, Pallas kernels, call(): pl.pallas_call(kernel, out_shape=out_shape, in_specs=[pl.BlockSpec(memory...  36 us
    ppermute x10, waiting for transfers between devices, pair(): return lax.ppermute(value, ('row', 'col'), ups + [(j, i) for i, j in ups])  23.5 us
    ppermute x10, starting transfers between devices, pair(): return lax.ppermute(value, ('row', 'col'), ups + [(j, i) for i, j in ups])  17.8 us
    ppermute x4, starting transfers between devices, cross(): return lax.ppermute(value, 'col', [(0, 1), (1, 0)])  2.46 us
  transfers between devices with their start and end apart: 14, of which 9 were waited for; matrix products, arithmetic and copies ran while one was open for 0% of the time, Pallas kernels for 26%

profile of v2, /device:TPU:9, one launch (start us, length us, event | category | flops | bytes accessed | tf_op | source)
XLA Modules:
  0.0 81.4 jit_solution(5953444368943367678)
XLA Ops:
  0.0 1.1 %shard_map.46 = (bf16[16,16,384]{2,1,0:T(8,128)(2,1)S(1)}, bf16[3,64,384]{2,1,0:T(8,128)(2,1)S(1)}, bf16[3,64,384]{2,1,0:T(8,128)(2,1)S(1)}) custom-call(bf16[16,64,384]{2,1,0:T(8,128)(2,1)} %refs_0_.1), custom_call_target="tpu_custom_call" | custom-call | flops 1 | tf_op jit(solution)/shard_map/pallas_call | solution.py:381
  1.1 1.3 %collective-permute-start.2 = (bf16[16,16,384]{2,1,0:T(8,128)(2,1)S(1)}, bf16[16,16,384]{2,1,0:T(8,128)(2,1)S(1)}, u32[]{:S(2)}, u32[]{:S(2)}) collective-permute-start(bf16[16,16,384]{2,1,0:T(8,128)(2,1)S(1)} %get-tuple-element.44), channel_id=1, source_target_pairs={{0,1},{1,0},{2,3},{3,2},{4,5},{5,4},{6,7},{7,6},{8,9},{9,8},{10,11... | collective-permute-start | bytes 589832 | tf_op jit(solution)/shard_map/ppermute | solution.py:499
  2.4 1.0 %collective-permute-start = (bf16[3,64,384]{2,1,0:T(8,128)(2,1)S(1)}, bf16[3,64,384]{2,1,0:T(8,128)(2,1)S(1)}, u32[]{:S(2)}, u32[]{:S(2)}) collective-permute-start(bf16[3,64,384]{2,1,0:T(8,128)(2,1)S(1)} %get-tuple-element.42), channel_id=1, source_target_pairs={{0,2},{1,3},{4,6},{5,7},{8,10},{9,11},{12,14},{13,15},{16,18},{17,... | collective-permute-start | bytes 442376 | tf_op jit(solution)/shard_map/ppermute | solution.py:478
  3.3 3.0 %collective-permute-start.1 = (bf16[3,64,384]{2,1,0:T(8,128)(2,1)S(1)}, bf16[3,64,384]{2,1,0:T(8,128)(2,1)S(1)}, u32[]{:S(2)}, u32[]{:S(2)}) collective-permute-start(bf16[3,64,384]{2,1,0:T(8,128)(2,1)S(1)} %get-tuple-element.43), channel_id=1, source_target_pairs={{2,4},{3,5},{6,8},{7,9},{10,12},{11,13},{14,16},{15,17},{18,20},{1... | collective-permute-start | bytes 442376 | tf_op jit(solution)/shard_map/ppermute | solution.py:478
  6.4 0.6 collective-permute-done.2.refs_1_
  7.0 3.5 %shard_map.47 = (f32[16,80,384]{2,1,0:T(8,128)S(1)}, bf16[16,80,1152]{2,1,0:T(8,128)(2,1)S(1)}, bf16[3456,384]{1,0:T(8,128)(2,1)S(1)}, f32[5,384]{1,0:T(8,128)S(1)}) custom-call(bf16[16,64,384]{2,1,0:T(8,128)(2,1)} %refs_0_.1, bf16[16,16,384]{2,1,0:T(8,128)(2,1)S(1)} %collective-permute-done.2.refs_1_, f32[5,384]{1,0:T(8,128)} %refs_2_.1, ...), custom_call_target="tpu_custom_call" | custom-call | flops 1698693120 | tf_op jit(solution)/shard_map/pallas_call | solution.py:381
  10.5 0.9 %collective-permute-done.1.two.refs_1_ = bf16[3,64,384]{2,1,0:T(8,128)(2,1)S(1)} collective-permute-done((bf16[3,64,384]{2,1,0:T(8,128)(2,1)S(1)}, bf16[3,64,384]{2,1,0:T(8,128)(2,1)S(1)}, u32[]{:S(2)}, u32[]{:S(2)}) %collective-permute-start.1) | collective-permute-done | bytes 147488 | tf_op jit(solution)/shard_map/ppermute | solution.py:478
  11.8 4.2 %shard_map.49 = (f32[12,80,384]{2,1,0:T(8,128)S(1)}, bf16[12,80,384]{2,1,0:T(8,128)(2,1)S(1)}, bf16[3456,384]{1,0:T(8,128)(2,1)S(1)}) custom-call(f32[16,80,384]{2,1,0:T(8,128)S(1)} %get-tuple-element.46.base.refs_6_, bf16[16,80,1152]{2,1,0:T(8,128)(2,1)S(1)} %get-tuple-element.45.after.taps.refs_5_, bf16[3456,384]{1,0:T(8,128)(2,1)S(1)} %get-tuple-element.47.w_one.refs_7_, ...), custom_call_target="tpu_custom_call" | custom-call | flops 2548039680 | tf_op jit(solution)/shard_map/pallas_call | solution.py:381
  16.0 9.3 %shard_map.50 = (f32[16,80,384]{2,1,0:T(8,128)S(1)}, bf16[16,80,1152]{2,1,0:T(8,128)(2,1)S(1)}, bf16[4,80,384]{2,1,0:T(8,128)(2,1)S(1)}, bf16[4,80,384]{2,1,0:T(8,128)(2,1)S(1)}, bf16[3456,384]{1,0:T(8,128)(2,1)S(1)}) custom-call(bf16[3,64,384]{2,1,0:T(8,128)(2,1)S(1)} %collective-permute-done.one.refs_0_, ...), custom_call_target="tpu_custom_call" | custom-call | flops 5096079360 | tf_op jit(solution)/shard_map/pallas_call | solution.py:381
  25.3 1.9 %collective-permute-start.4 = (bf16[4,80,384]{2,1,0:T(8,128)(2,1)S(1)}, bf16[4,80,384]{2,1,0:T(8,128)(2,1)S(1)}, u32[]{:S(2)}, u32[]{:S(2)}) collective-permute-start(bf16[4,80,384]{2,1,0:T(8,128)(2,1)S(1)} %get-tuple-element.52), channel_id=1, source_target_pairs={{0,2},{1,3},{4,6},{5,7},{8,10},{9,11},{12,14},{13,15},{16,18},{17,... | collective-permute-start | bytes 737288 | tf_op jit(solution)/shard_map/ppermute | solution.py:478
  27.2 3.2 %collective-permute-start.5 = (bf16[4,80,384]{2,1,0:T(8,128)(2,1)S(1)}, bf16[4,80,384]{2,1,0:T(8,128)(2,1)S(1)}, u32[]{:S(2)}, u32[]{:S(2)}) collective-permute-start(bf16[4,80,384]{2,1,0:T(8,128)(2,1)S(1)} %get-tuple-element.53), channel_id=1, source_target_pairs={{2,4},{3,5},{6,8},{7,9},{10,12},{11,13},{14,16},{15,17},{18,20},{1... | collective-permute-start | bytes 737288 | tf_op jit(solution)/shard_map/ppermute | solution.py:478
  30.5 5.2 %shard_map.51 = (f32[8,80,384]{2,1,0:T(8,128)S(1)}, f32[8,64,384]{2,1,0:T(8,128)S(1)}, bf16[8,72,384]{2,1,0:T(8,128)(2,1)S(1)}, bf16[3456,384]{1,0:T(8,128)(2,1)S(1)}) custom-call(bf16[16,80,1152]{2,1,0:T(8,128)(2,1)S(1)} %get-tuple-element.54.taps, bf16[3456,384]{1,0:T(8,128)(2,1)S(1)} %get-tuple-element.55.weight, bf16[4,3456,384]{2,1,0:T(8,128)(2,1)} %bitcast.4, ...), custom_call_target="tpu_custom_call" | custom-call | flops 3397386240 | tf_op jit(solution)/shard_map/pallas_call | solution.py:381
  35.6 1.7 %collective-permute-done.5.got_two = bf16[4,80,384]{2,1,0:T(8,128)(2,1)S(1)} collective-permute-done((bf16[4,80,384]{2,1,0:T(8,128)(2,1)S(1)}, bf16[4,80,384]{2,1,0:T(8,128)(2,1)S(1)}, u32[]{:S(2)}, u32[]{:S(2)}) %collective-permute-start.5) | collective-permute-done | bytes 245792 | tf_op jit(solution)/shard_map/ppermute | solution.py:478
  37.4 2.1 %shard_map.52 = (f32[16,64,384]{2,1,0:T(8,128)S(1)}, bf16[16,72,384]{2,1,0:T(8,128)(2,1)S(1)}, bf16[8,72,384]{2,1,0:T(8,128)(2,1)S(1)}, bf16[8,72,384]{2,1,0:T(8,128)(2,1)S(1)}) custom-call(bf16[4,80,384]{2,1,0:T(8,128)(2,1)S(1)} %collective-permute-done.4.got_one, bf16[4,80,384]{2,1,0:T(8,128)(2,1)S(1)} %collective-permute-done.5.got_two, ...), custom_call_target="tpu_custom_call" | custom-call | flops 566231040 | tf_op jit(solution)/shard_map/pallas_call | solution.py:381
  39.5 3.1 %collective-permute-start.8 = (bf16[8,72,384]{2,1,0:T(8,128)(2,1)S(1)}, bf16[8,72,384]{2,1,0:T(8,128)(2,1)S(1)}, u32[]{:S(2)}, u32[]{:S(2)}) collective-permute-start(bf16[8,72,384]{2,1,0:T(8,128)(2,1)S(1)} %get-tuple-element.65), channel_id=1, source_target_pairs={{2,4},{3,5},{6,8},{7,9},{10,12},{11,13},{14,16},{15,17},{18,20},{1... | collective-permute-start | bytes 1327112 | tf_op jit(solution)/shard_map/ppermute | solution.py:478
  42.6 3.1 %shard_map.53.acc = f32[16,64,384]{2,1,0:T(8,128)S(1)} custom-call(bf16[16,72,384]{2,1,0:T(8,128)(2,1)S(1)} %get-tuple-element.61.act, bf16[3456,384]{1,0:T(8,128)(2,1)S(1)} %get-tuple-element.62.weight, f32[16,64,384]{2,1,0:T(8,128)S(1)} %get-tuple-element.63.stream), custom_call_target="tpu_custom_call" | custom-call | flops 2717908992 | tf_op jit(solution)/shard_map/pallas_call | solution.py:381
  45.7 1.4 %shard_map.54 = (f32[8,64,384]{2,1,0:T(8,128)S(1)}, bf16[8,64,384]{2,1,0:T(8,128)(2,1)S(1)}) custom-call(bf16[8,72,384]{2,1,0:T(8,128)(2,1)S(1)} %collective-permute-done.6.got, f32[16,64,384]{2,1,0:T(8,128)S(1)} %shard_map.53.acc, bf16[3456,384]{1,0:T(8,128)(2,1)S(1)} %get-tuple-element.62.weight, f32[5,384]{1,0:T(8,128)S(1)} %get-tuple-element.48.gains.refs_10_), custom_call_target="tpu_custom_call" | custom-call | flops 452984832 | tf_op jit(solution)/shard_map/pallas_call | solution.py:381
  47.1 0.4 collective-permute-start.7
  47.5 6.7 %collective-permute-done.8.got = bf16[8,72,384]{2,1,0:T(8,128)(2,1)S(1)} collective-permute-done((bf16[8,72,384]{2,1,0:T(8,128)(2,1)S(1)}, bf16[8,72,384]{2,1,0:T(8,128)(2,1)S(1)}, u32[]{:S(2)}, u32[]{:S(2)}) %collective-permute-start.8) | collective-permute-done | bytes 442400 | tf_op jit(solution)/shard_map/ppermute | solution.py:478
  54.2 1.4 %shard_map.55 = (f32[8,64,384]{2,1,0:T(8,128)S(1)}, bf16[8,64,384]{2,1,0:T(8,128)(2,1)S(1)}) custom-call(bf16[8,72,384]{2,1,0:T(8,128)(2,1)S(1)} %collective-permute-done.8.got, f32[16,64,384]{2,1,0:T(8,128)S(1)} %shard_map.53.acc, bf16[3456,384]{1,0:T(8,128)(2,1)S(1)} %get-tuple-element.62.weight, f32[5,384]{1,0:T(8,128)S(1)} %get-tuple-element.48.gains.refs_10_), custom_call_target="tpu_custom_call" | custom-call | flops 452984832 | tf_op jit(solution)/shard_map/pallas_call | solution.py:381
  55.5 3.4 %collective-permute-start.10 = (bf16[8,64,384]{2,1,0:T(8,128)(2,1)S(1)}, bf16[8,64,384]{2,1,0:T(8,128)(2,1)S(1)}, u32[]{:S(2)}, u32[]{:S(2)}) collective-permute-start(bf16[8,64,384]{2,1,0:T(8,128)(2,1)S(1)} %get-tuple-element.66.b), channel_id=1, source_target_pairs={{8,16},{9,17},{10,18},{11,19},{12,20},{13,21},{14,22},{15,23},{16,... | collective-permute-start | bytes 1179656 | tf_op jit(solution)/shard_map/ppermute | solution.py:478
  59.1 0.7 shard_map.57
  59.7 0.9 %shard_map.56 = (f32[8,64,384]{2,1,0:T(8,128)S(1)}, f32[8,64,384]{2,1,0:T(8,128)S(1)}, f32[8,64,384]{2,1,0:T(8,128)S(1)}) custom-call(bf16[8,64,384]{2,1,0:T(8,128)(2,1)S(1)} %get-tuple-element.64.a, bf16[3,3,384,384]{3,2,1,0:T(8,128)(2,1)S(1)} %copy-done, f32[8,64,384]{2,1,0:T(8,128)S(1)} %get-tuple-element.67.stream), custom_call_target="tpu_custom_call" | custom-call | flops 452984832 | tf_op jit(solution)/shard_map/pallas_call | solution.py:381
  60.6 4.6 %collective-permute-done.10.refs_2_ = bf16[8,64,384]{2,1,0:T(8,128)(2,1)S(1)} collective-permute-done((bf16[8,64,384]{2,1,0:T(8,128)(2,1)S(1)}, bf16[8,64,384]{2,1,0:T(8,128)(2,1)S(1)}, u32[]{:S(2)}, u32[]{:S(2)}) %collective-permute-start.10) | collective-permute-done | bytes 393248 | tf_op jit(solution)/shard_map/ppermute | solution.py:478
  65.2 1.9 %collective-permute-done.9.refs_1_ = bf16[8,64,384]{2,1,0:T(8,128)(2,1)S(1)} collective-permute-done((bf16[8,64,384]{2,1,0:T(8,128)(2,1)S(1)}, bf16[8,64,384]{2,1,0:T(8,128)(2,1)S(1)}, u32[]{:S(2)}, u32[]{:S(2)}) %collective-permute-start.9) | collective-permute-done | bytes 393248 | tf_op jit(solution)/shard_map/ppermute | solution.py:478
  67.1 1.1 %shard_map.59 = (bf16[8,64,384]{2,1,0:T(8,128)(2,1)S(1)}, bf16[8,64,384]{2,1,0:T(8,128)(2,1)S(1)}, bf16[8,64,384]{2,1,0:T(8,128)(2,1)S(1)}) custom-call(bf16[8,64,384]{2,1,0:T(8,128)(2,1)S(1)} %collective-permute-done.7.refs_0_, bf16[8,64,384]{2,1,0:T(8,128)(2,1)S(1)} %collective-permute-done.9.refs_1_, ...), custom_call_target="tpu_custom_call" | custom-call | flops 603979776 | tf_op jit(solution)/shard_map/pallas_call | solution.py:381
  68.3 2.1 %collective-permute-start.12 = (bf16[8,64,384]{2,1,0:T(8,128)(2,1)S(1)}, bf16[8,64,384]{2,1,0:T(8,128)(2,1)S(1)}, u32[]{:S(2)}, u32[]{:S(2)}) collective-permute-start(bf16[8,64,384]{2,1,0:T(8,128)(2,1)S(1)} %get-tuple-element.77), channel_id=1, source_target_pairs={{8,16},{9,17},{10,18},{11,19},{12,20},{13,21},{14,22},{15,23},{16,... | collective-permute-start | bytes 1179656 | tf_op jit(solution)/shard_map/ppermute | solution.py:478
  70.8 0.9 %shard_map.58 = (f32[8,64,384]{2,1,0:T(8,128)S(1)}, f32[8,64,384]{2,1,0:T(8,128)S(1)}) custom-call(bf16[8,64,384]{2,1,0:T(8,128)(2,1)S(1)} %collective-permute-done.7.refs_0_, bf16[8,64,384]{2,1,0:T(8,128)(2,1)S(1)} %collective-permute-done.9.refs_1_, bf16[8,64,384]{2,1,0:T(8,128)(2,1)S(1)} %collective-permute-done.10.refs_2_, ...), custom_call_target="tpu_custom_call" | custom-call | flops 452984832 | tf_op jit(solution)/shard_map/pallas_call | solution.py:381
  71.7 6.1 %collective-permute-done.11.back_one = bf16[8,64,384]{2,1,0:T(8,128)(2,1)S(1)} collective-permute-done((bf16[8,64,384]{2,1,0:T(8,128)(2,1)S(1)}, bf16[8,64,384]{2,1,0:T(8,128)(2,1)S(1)}, u32[]{:S(2)}, u32[]{:S(2)}) %collective-permute-start.11) | collective-permute-done | bytes 393248 | tf_op jit(solution)/shard_map/ppermute | solution.py:478
  77.8 1.6 %collective-permute-done.12.back_two = bf16[8,64,384]{2,1,0:T(8,128)(2,1)S(1)} collective-permute-done((bf16[8,64,384]{2,1,0:T(8,128)(2,1)S(1)}, bf16[8,64,384]{2,1,0:T(8,128)(2,1)S(1)}, u32[]{:S(2)}, u32[]{:S(2)}) %collective-permute-start.12) | collective-permute-done | bytes 393248 | tf_op jit(solution)/shard_map/ppermute | solution.py:478
  79.4 0.5 collective-permute-done.13.refs_0_
  79.9 1.3 %shard_map.60 = f32[16,64,384]{2,1,0:T(8,128)} custom-call(f32[8,64,384]{2,1,0:T(8,128)S(1)} %get-tuple-element.71.own_a, f32[8,64,384]{2,1,0:T(8,128)S(1)} %get-tuple-element.72.own_b, bf16[8,64,384]{2,1,0:T(8,128)(2,1)S(1)} %collective-permute-done.11.back_one, bf16[8,64,384]{2,1,0:T(8,128)(2,1)S(1)} %collective-permute-done.12.back_two, ...), custom_call_target="tpu_custom_call" | custom-call | flops 1 | tf_op jit(solution)/shard_map/pallas_call | solution.py:381
  (13 shorter events, 1.0 us)
Async XLA Ops:
  1.1 5.9 %collective-permute-start.2 = (bf16[16,16,384]{2,1,0:T(8,128)(2,1)S(1)}, bf16[16,16,384]{2,1,0:T(8,128)(2,1)S(1)}, u32[]{:S(2)}, u32[]{:S(2)}) collective-permute-start(bf16[16,16,384]{2,1,0:T(8,128)(2,1)S(1)} %get-tuple-element.44), channel_id=1, source_target_pairs={{0,1},{1,0},{2,3},{3,2},{4,5},{5,4},{6,7},{7,6},{8,9},{9,8},{10,11... | collective-permute-start | bytes 589832 | tf_op jit(solution)/shard_map/ppermute | solution.py:499
  2.4 8.1 %collective-permute-start = (bf16[3,64,384]{2,1,0:T(8,128)(2,1)S(1)}, bf16[3,64,384]{2,1,0:T(8,128)(2,1)S(1)}, u32[]{:S(2)}, u32[]{:S(2)}) collective-permute-start(bf16[3,64,384]{2,1,0:T(8,128)(2,1)S(1)} %get-tuple-element.42), channel_id=1, source_target_pairs={{0,2},{1,3},{4,6},{5,7},{8,10},{9,11},{12,14},{13,15},{16,18},{17,... | collective-permute-start | bytes 442376 | tf_op jit(solution)/shard_map/ppermute | solution.py:478
  3.3 8.0 %collective-permute-start.1 = (bf16[3,64,384]{2,1,0:T(8,128)(2,1)S(1)}, bf16[3,64,384]{2,1,0:T(8,128)(2,1)S(1)}, u32[]{:S(2)}, u32[]{:S(2)}) collective-permute-start(bf16[3,64,384]{2,1,0:T(8,128)(2,1)S(1)} %get-tuple-element.43), channel_id=1, source_target_pairs={{2,4},{3,5},{6,8},{7,9},{10,12},{11,13},{14,16},{15,17},{18,20},{1... | collective-permute-start | bytes 442376 | tf_op jit(solution)/shard_map/ppermute | solution.py:478
  11.4 4.6 %collective-permute-start.3 = (bf16[6,16,384]{2,1,0:T(8,128)(2,1)S(1)}, bf16[6,16,384]{2,1,0:T(8,128)(2,1)S(1)}, u32[]{:S(2)}, u32[]{:S(2)}) collective-permute-start(bf16[6,16,384]{2,1,0:T(8,128)(2,1)S(1)} %shard_map.48), channel_id=1, source_target_pairs={{0,1},{1,0},{2,3},{3,2},{4,5},{5,4},{6,7},{7,6},{8,9},{9,8},{10,11... | collective-permute-start | bytes 221192 | tf_op jit(solution)/shard_map/ppermute | solution.py:499
  25.3 10.3 %collective-permute-start.4 = (bf16[4,80,384]{2,1,0:T(8,128)(2,1)S(1)}, bf16[4,80,384]{2,1,0:T(8,128)(2,1)S(1)}, u32[]{:S(2)}, u32[]{:S(2)}) collective-permute-start(bf16[4,80,384]{2,1,0:T(8,128)(2,1)S(1)} %get-tuple-element.52), channel_id=1, source_target_pairs={{0,2},{1,3},{4,6},{5,7},{8,10},{9,11},{12,14},{13,15},{16,18},{17,... | collective-permute-start | bytes 737288 | tf_op jit(solution)/shard_map/ppermute | solution.py:478
  27.2 10.1 %collective-permute-start.5 = (bf16[4,80,384]{2,1,0:T(8,128)(2,1)S(1)}, bf16[4,80,384]{2,1,0:T(8,128)(2,1)S(1)}, u32[]{:S(2)}, u32[]{:S(2)}) collective-permute-start(bf16[4,80,384]{2,1,0:T(8,128)(2,1)S(1)} %get-tuple-element.53), channel_id=1, source_target_pairs={{2,4},{3,5},{6,8},{7,9},{10,12},{11,13},{14,16},{15,17},{18,20},{1... | collective-permute-start | bytes 737288 | tf_op jit(solution)/shard_map/ppermute | solution.py:478
  39.4 6.2 %collective-permute-start.6 = (bf16[8,72,384]{2,1,0:T(8,128)(2,1)S(1)}, bf16[8,72,384]{2,1,0:T(8,128)(2,1)S(1)}, u32[]{:S(2)}, u32[]{:S(2)}) collective-permute-start(bf16[8,72,384]{2,1,0:T(8,128)(2,1)S(1)} %get-tuple-element.60), channel_id=1, source_target_pairs={{0,2},{1,3},{4,6},{5,7},{8,10},{9,11},{12,14},{13,15},{16,18},{17,... | collective-permute-start | bytes 1327112 | tf_op jit(solution)/shard_map/ppermute | solution.py:478
  39.5 14.7 %collective-permute-start.8 = (bf16[8,72,384]{2,1,0:T(8,128)(2,1)S(1)}, bf16[8,72,384]{2,1,0:T(8,128)(2,1)S(1)}, u32[]{:S(2)}, u32[]{:S(2)}) collective-permute-start(bf16[8,72,384]{2,1,0:T(8,128)(2,1)S(1)} %get-tuple-element.65), channel_id=1, source_target_pairs={{2,4},{3,5},{6,8},{7,9},{10,12},{11,13},{14,16},{15,17},{18,20},{1... | collective-permute-start | bytes 1327112 | tf_op jit(solution)/shard_map/ppermute | solution.py:478
  47.1 12.0 %copy-start = (bf16[3,3,384,384]{3,2,1,0:T(8,128)(2,1)S(1)}, bf16[3,3,384,384]{3,2,1,0:T(8,128)(2,1)}, u32[]{:S(2)}) copy-start(bf16[3,3,384,384]{3,2,1,0:T(8,128)(2,1)} %refs_3_.3) | copy-start | bytes 7962628
  47.1 13.6 %collective-permute-start.7 = (bf16[8,64,384]{2,1,0:T(8,128)(2,1)S(1)}, bf16[8,64,384]{2,1,0:T(8,128)(2,1)S(1)}, u32[]{:S(2)}, u32[]{:S(2)}) collective-permute-start(bf16[8,64,384]{2,1,0:T(8,128)(2,1)S(1)} %get-tuple-element.64.a), channel_id=1, source_target_pairs={{0,1},{1,0},{2,3},{3,2},{4,5},{5,4},{6,7},{7,6},{8,9},{9,8},{10,11... | collective-permute-start | bytes 1179656 | tf_op jit(solution)/shard_map/ppermute | solution.py:499
  55.5 9.6 %collective-permute-start.10 = (bf16[8,64,384]{2,1,0:T(8,128)(2,1)S(1)}, bf16[8,64,384]{2,1,0:T(8,128)(2,1)S(1)}, u32[]{:S(2)}, u32[]{:S(2)}) collective-permute-start(bf16[8,64,384]{2,1,0:T(8,128)(2,1)S(1)} %get-tuple-element.66.b), channel_id=1, source_target_pairs={{8,16},{9,17},{10,18},{11,19},{12,20},{13,21},{14,22},{15,23},{16,... | collective-permute-start | bytes 1179656 | tf_op jit(solution)/shard_map/ppermute | solution.py:478
  59.0 8.1 %collective-permute-start.9 = (bf16[8,64,384]{2,1,0:T(8,128)(2,1)S(1)}, bf16[8,64,384]{2,1,0:T(8,128)(2,1)S(1)}, u32[]{:S(2)}, u32[]{:S(2)}) collective-permute-start(bf16[8,64,384]{2,1,0:T(8,128)(2,1)S(1)} %get-tuple-element.66.b), channel_id=1, source_target_pairs={{0,8},{1,9},{2,10},{3,11},{4,12},{5,13},{6,14},{7,15},{16,24},{17,... | collective-permute-start | bytes 1179656 | tf_op jit(solution)/shard_map/ppermute | solution.py:478
  68.2 9.5 %collective-permute-start.11 = (bf16[8,64,384]{2,1,0:T(8,128)(2,1)S(1)}, bf16[8,64,384]{2,1,0:T(8,128)(2,1)S(1)}, u32[]{:S(2)}, u32[]{:S(2)}) collective-permute-start(bf16[8,64,384]{2,1,0:T(8,128)(2,1)S(1)} %get-tuple-element.76), channel_id=1, source_target_pairs={{0,8},{1,9},{2,10},{3,11},{4,12},{5,13},{6,14},{7,15},{16,24},{17,... | collective-permute-start | bytes 1179656 | tf_op jit(solution)/shard_map/ppermute | solution.py:478
  68.3 11.1 %collective-permute-start.12 = (bf16[8,64,384]{2,1,0:T(8,128)(2,1)S(1)}, bf16[8,64,384]{2,1,0:T(8,128)(2,1)S(1)}, u32[]{:S(2)}, u32[]{:S(2)}) collective-permute-start(bf16[8,64,384]{2,1,0:T(8,128)(2,1)S(1)} %get-tuple-element.77), channel_id=1, source_target_pairs={{8,16},{9,17},{10,18},{11,19},{12,20},{13,21},{14,22},{15,23},{16,... | collective-permute-start | bytes 1179656 | tf_op jit(solution)/shard_map/ppermute | solution.py:478
  70.4 9.5 %collective-permute-start.13 = (bf16[8,64,384]{2,1,0:T(8,128)(2,1)S(1)}, bf16[8,64,384]{2,1,0:T(8,128)(2,1)S(1)}, u32[]{:S(2)}, u32[]{:S(2)}) collective-permute-start(bf16[8,64,384]{2,1,0:T(8,128)(2,1)S(1)} %get-tuple-element.78), channel_id=1, source_target_pairs={{0,1},{1,0},{2,3},{3,2},{4,5},{5,4},{6,7},{7,6},{8,9},{9,8},{10,11... | collective-permute-start | bytes 1179656 | tf_op jit(solution)/shard_map/ppermute | solution.py:499
